TPU v7x, 256 devices: a 2x2x32 block of a 4x8x32 slice. The times are simulated.
256 devices in a mesh: groups: 4 (over x, y), ctx: 64 (over z, core).
Axes of the slice: x: 2, y: 2, z: 32, core: 2. Of those that a mesh axis runs over, the one named last changes fastest.
The devices are a block of a 4x8x32 slice.
Arguments:
- queries: bfloat16 [1024, 8192], P(('groups', 'ctx')), parts along dimension 0, may hold values from -200 to 200
- new_kv: bfloat16 [1024, 1024], P(('groups', 'ctx')), parts along dimension 0, may hold values from -9 to 9
- prefix_cache: bfloat16 [262144, 1024], P(('groups', 'ctx')), parts along dimension 0, may hold values from -6.5 to 6.5
- positions: int32 [1024], P('groups'), parts along dimension 0, may hold values from 0 to 255, each once
- lengths: int32 [256], P('groups'), parts along dimension 0, may hold values from 1 to 1024, 49152 in all
- out_weight: bfloat16 [8192, 16384], P(None, 'ctx'), may hold values from -0.0625 to 0.0625
Outputs:
- attended: bfloat16 [1024, 8192], P(('groups', 'ctx')), parts along dimension 0
- projected: bfloat16 [1024, 16384], P('groups', 'ctx'), parts along dimension 0
There are 4 independent parts, one for each index of `groups`. A program takes and returns all parts, laid end to end along the dimension named above; an argument that names none is the same for every part. Nothing has to cross between parts.
Inputs may be any that keep to these rules, and one draw needn't show every extreme that they name: `positions`: a permutation of 0 to 255. The filled slots of shard i are its first lengths[i] slots; they sum to 49152, and some shard is full.
All inputs are finite; a program needn't handle non-finite values.
Results may differ from a plain program's by a relative error of at most 0.0045.
Values may be sent and summed in bfloat16 or wider, within the bound.
No kernel may reach another device: no remote copies, remote signals or barrier semaphores. Data moves between devices by JAX's collectives and lax.ppermute only.
A program may use at most 128 MiB of HBM per device.

v0:
```python
import functools
import math

import jax
import jax.numpy as jnp
from jax import lax
from jax.experimental import pallas as pl
from jax.experimental.pallas import tpu as pltpu
from jax.sharding import PartitionSpec as P

HQ = 64
KVH = 4
HD = 128
CTX = "ctx"
SPREAD = ("groups", "ctx")
TILE = 4
HOP = 4
TAIL = 16
ROWS = HD + TAIL
DEAD = -1e30
TO_LOG2 = math.log2(math.e) / math.sqrt(HD)


def prepare_body(lens_ref, mine_k, mine_v, theirs_k, theirs_v, keys_out, values_out):
    slots = mine_k.shape[0]
    lane = lax.broadcasted_iota(jnp.int32, (slots, HD), 1)
    row = lax.broadcasted_iota(jnp.int32, (slots, HD), 0)
    for half, (k_ref, v_ref) in enumerate(((mine_k, mine_v), (theirs_k, theirs_v))):
        dead = jnp.where((lane == 0) & (row >= lens_ref[half + 1]), DEAD, 0.0)
        span = pl.ds(half * slots, slots)
        keys_out[0, span, :HD] = k_ref[...]
        keys_out[0, span, HD:] = dead.astype(jnp.bfloat16)
        values_out[0, :, span] = v_ref[...].T


def prepare(core_lens, cache, theirs):
    slots = cache.shape[0]
    mine = lambda part: pl.BlockSpec((slots, HD), lambda g, s: (0, s[0] * KVH + 2 * g + part))
    return pl.pallas_call(
        prepare_body,
        grid_spec=pltpu.PrefetchScalarGridSpec(
            num_scalar_prefetch=1,
            grid=(KVH // 2,),
            in_specs=[mine(0), mine(1), mine(0), mine(1)],
            out_specs=[
                pl.BlockSpec((1, 2 * slots, 2 * HD), lambda g, s: (g, 0, 0)),
                pl.BlockSpec((1, HD, 2 * slots), lambda g, s: (g, 0, 0)),
            ],
        ),
        out_shape=[
            jax.ShapeDtypeStruct((KVH // 2, 2 * slots, 2 * HD), jnp.bfloat16),
            jax.ShapeDtypeStruct((KVH // 2, HD, 2 * slots), jnp.bfloat16),
        ],
        cost_estimate=pl.CostEstimate(flops=slots * HD * 2048, transcendentals=0, bytes_accessed=10 * slots * HD * KVH),
        name="prepare",
    )(core_lens, cache, cache, theirs, theirs)


def tail_rows(level):
    first = level.astype(jnp.bfloat16).astype(jnp.float32)
    second = (level - first).astype(jnp.bfloat16).astype(jnp.float32)
    third = level - first - second
    row = lax.broadcasted_iota(jnp.int32, (TAIL, level.shape[1]), 0)
    wide = jnp.where(row == 0, first, jnp.where(row == 1, second, jnp.where(row == 2, third, 0.0)))
    return wide.astype(jnp.bfloat16)


def level_of(tail):
    wide = tail.astype(jnp.float32)
    return wide[0:1] + wide[1:2] + wide[2:3]


def attend_body(pos_new, keys_ref, values_ref, new_k, new_v, *refs):
    count = len(refs) // 3
    nt = (((1,), (1,)), ((), ()))
    tn = (((0,), (0,)), ((), ()))

    def softmax(s):
        top = jnp.max(s, axis=0, keepdims=True)
        p = jnp.exp2((s - top) * TO_LOG2)
        return top, jnp.sum(p, axis=0, keepdims=True), p.astype(jnp.bfloat16)

    for q_ref, pos_ref, out_ref in zip(refs[:count], refs[count : 2 * count], refs[2 * count :]):

        def tile(i, carry, q_ref=q_ref, pos_ref=pos_ref, out_ref=out_ref):
            base = i * TILE
            q = jnp.concatenate([q_ref[base + k, 0] for k in range(TILE)], axis=0)
            at = jnp.concatenate([pos_ref[base + k] for k in range(TILE)], axis=1)
            lane = lax.broadcasted_iota(jnp.int32, q.shape, 1)
            q_wide = jnp.concatenate([q, jnp.where(lane == 0, 1.0, 0.0).astype(q.dtype)], axis=1)
            s = lax.dot_general(keys_ref[0], q_wide, nt, preferred_element_type=jnp.float32)
            top_a, total_a, p = softmax(s)
            out_a = jnp.dot(values_ref[0], p, preferred_element_type=jnp.float32)
            s = lax.dot_general(new_k[0], q, nt, preferred_element_type=jnp.float32)
            top_b, total_b, p = softmax(jnp.where(at >= pos_new[...], s, DEAD))
            out_b = lax.dot_general(new_v[0], p, tn, preferred_element_type=jnp.float32)
            best = jnp.maximum(top_a, top_b)
            keep_a = jnp.exp2((top_a - best) * TO_LOG2)
            keep_b = jnp.exp2((top_b - best) * TO_LOG2)
            total = keep_a * total_a + keep_b * total_b
            out = (keep_a * out_a + keep_b * out_b) * (1.0 / total)
            out = out.astype(jnp.bfloat16)
            tail = tail_rows(best * TO_LOG2 + jnp.log2(total))
            for k in range(TILE):
                lanes = slice(k * HD, (k + 1) * HD)
                out_ref[base + k, 0, :HD, :] = out[:, lanes]
                out_ref[base + k, 0, HD:, :] = tail[:, lanes]
            return carry

        if q_ref.shape[0] == TILE:
            tile(0, 0)
        else:
            lax.fori_loop(0, q_ref.shape[0] // TILE, tile, 0)


def attend(prepared, pos_new, new_k, new_v, blocks, places):
    keys, values = prepared
    per_group = lambda a: pl.BlockSpec((1, *a.shape[1:]), lambda g: (g, 0, 0))
    whole = lambda a: pl.BlockSpec(a.shape, lambda g: (0,) * a.ndim)
    one = lambda a, rows: pl.BlockSpec((a.shape[0], 1, rows, HD), lambda g: (0, g, 0, 0))
    score_count = sum(b.shape[0] for b in blocks) * HD * keys.shape[0] * keys.shape[1]
    return pl.pallas_call(
        attend_body,
        grid=(KVH // 2,),
        in_specs=[whole(pos_new), per_group(keys), per_group(values), per_group(new_k), per_group(new_v)]
        + [one(b, HD) for b in blocks]
        + [whole(p) for p in places],
        out_specs=[one(b, ROWS) for b in blocks],
        out_shape=[jax.ShapeDtypeStruct((b.shape[0], KVH // 2, ROWS, HD), jnp.bfloat16) for b in blocks],
        compiler_params=pltpu.CompilerParams(vmem_limit_bytes=48 * 1024 * 1024),
        cost_estimate=pl.CostEstimate(
            flops=score_count * 6 * HD,
            transcendentals=score_count,
            bytes_accessed=2 * (keys.size + values.size + 2 * sum(b.size for b in blocks)),
        ),
        name="attend",
    )(pos_new, keys, values, new_k, new_v, *blocks, *places)


def merged(parts):
    levels = [level_of(t) for _, t in parts]
    best = functools.reduce(jnp.maximum, levels)
    weights = [jnp.exp2(v - best) for v in levels]
    total = sum(weights)
    out = sum(w * o.astype(jnp.float32) for w, (o, _) in zip(weights, parts)) * (1.0 / total)
    return out, best + jnp.log2(total)


def merge_body(jobs, *refs):
    ins, outs = list(refs[: -len(jobs)]), refs[-len(jobs) :]
    for starts, out_ref in zip(jobs, outs):
        parts = [(ins.pop(0), b0, g0) for b0, g0 in starts]
        for g in range(out_ref.shape[1]):
            here = [(r, b0, g - g0) for r, b0, g0 in parts if 0 <= g - g0 < r.shape[1]]
            cuts = sorted({c for r, b0, _ in here for c in (b0, b0 + r.shape[0])})
            for low, high in zip(cuts[:-1], cuts[1:]):
                live = [(r, b0, k) for r, b0, k in here if b0 <= low and high <= b0 + r.shape[0]]

                def visit(b, carry, live=live, g=g, out_ref=out_ref):
                    if len(live) == 1:
                        r, b0, k = live[0]
                        out_ref[b, g] = r[b - b0, k]
                        return carry
                    out, level = merged(
                        [(r[b - b0, k, :HD, :], r[b - b0, k, HD:, :]) for r, b0, k in live]
                    )
                    out_ref[b, g, :HD, :] = out.astype(jnp.bfloat16)
                    out_ref[b, g, HD:, :] = tail_rows(level)
                    return carry

                if high - low == 1:
                    visit(low, 0)
                else:
                    lax.fori_loop(low, high, visit, 0)


def merge(*jobs):
    arrays = [a for job in jobs for a, _, _ in job]
    starts = tuple(tuple((b0, g0) for _, b0, g0 in job) for job in jobs)
    return pl.pallas_call(
        functools.partial(merge_body, starts),
        out_shape=[jax.ShapeDtypeStruct(job[0][0].shape, job[0][0].dtype) for job in jobs],
        name="merge",
    )(*arrays)


def finish_body(parts_ref, out_ref):
    for g in range(out_ref.shape[0]):
        out, _ = merged([(parts_ref[k, g, :HD, :], parts_ref[k, g, HD:, :]) for k in range(parts_ref.shape[0])])
        out_ref[g] = out.T.astype(jnp.bfloat16)


def finish(parts):
    return pl.pallas_call(
        finish_body,
        out_shape=jax.ShapeDtypeStruct((KVH // 2, HD, HD), jnp.bfloat16),
        name="finish",
    )(parts)


def shards(queries, new_kv, prefix_cache, positions, lengths, out_weight):
    devices = lax.axis_size(CTX)
    chips = devices // 2
    ring = chips // HOP
    index = lax.axis_index(CTX)
    chip, core = index // 2, index % 2
    tokens = queries.shape[0]
    per_group = HQ // KVH
    half = HQ * HD // 2

    def take(x, d):
        return lax.ppermute(x, CTX, [(i, (i - 2 * d) % devices) for i in range(devices)])

    def swap(x):
        return lax.ppermute(x, CTX, [(i, i ^ 1) for i in range(devices)])

    def halves(x, axis):
        width = x.shape[axis] // 2
        keep = lax.dynamic_slice_in_dim(x, core * width, width, axis)
        send = lax.dynamic_slice_in_dim(x, (1 - core) * width, width, axis)
        return keep, send

    def in_order(mine, theirs):
        return jnp.where(core == 0, jnp.concatenate([mine, theirs]), jnp.concatenate([theirs, mine]))

    def after(first, *then):
        return lax.optimization_barrier((*then, first))[:-1]

    classes = [[2 * (b + HOP * a) + c for a in range(ring)] for b in range(HOP) for c in range(2)]

    def gathered(block, last=lambda own: ()):
        own = lax.all_gather(block, CTX, axis_index_groups=classes)
        right, left = take(own, 1), take(own, -1)
        done = last(own)
        right, left = after(done, right, left)
        return own, right, left, take(right[: ring // 2], 1), take(left[ring // 2 :], -1), done

    q_mine, q_send = halves(queries, 1)
    n_mine, n_send = halves(new_kv, 1)
    small = swap(jnp.concatenate([q_send, n_send], axis=1))
    theirs = swap(prefix_cache)
    q_block = in_order(q_mine, small[:, :half])
    q_block = q_block.reshape(2 * tokens, KVH // 2, per_group, HD).transpose(1, 0, 2, 3)
    q_block = q_block.reshape(KVH // 2, 2 * tokens * per_group, HD)
    new_rows = jnp.concatenate([n_mine, small[:, half:]])
    new_rows = jnp.pad(new_rows, ((0, TAIL - 2 * tokens), (0, 0))).reshape(TAIL, KVH // 2, 2, HD)
    new_k, new_v = new_rows[:, :, 0].transpose(1, 0, 2), new_rows[:, :, 1].transpose(1, 0, 2)
    pos_of = lambda who: lax.dynamic_slice_in_dim(positions, who * tokens, tokens, 0)
    pos_new = jnp.concatenate([pos_of(index), pos_of(index ^ 1)])
    pos_new = jnp.pad(pos_new, (0, TAIL - 2 * tokens), constant_values=positions.shape[0])[:, None]
    placed = jnp.repeat(positions.reshape(chips, 2 * tokens), per_group, axis=1)
    placed = placed.reshape(ring, HOP, 1, placed.shape[1])
    place = lambda r: lax.dynamic_index_in_dim(placed, (chip + r) % HOP, 1, keepdims=False)
    length_of = lambda who: lax.dynamic_index_in_dim(lengths, who, 0, keepdims=False)
    core_lens = jnp.stack([core, length_of(index), length_of(index ^ 1)]).astype(jnp.int32)
    prepared = prepare(core_lens, prefix_cache, theirs)
    w_mine = lax.dynamic_slice_in_dim(out_weight, core * half, half, 0)

    w_send = lax.dynamic_slice_in_dim(out_weight, (1 - core) * half, half, 0)
    w_theirs = swap(w_send)

    def score(blocks, places):
        return attend(prepared, pos_new, new_k, new_v, blocks, places)

    own, right, left, right_far, left_far, parts_own = gathered(q_block, lambda own: score([own], [place(0)]))
    parts_right = score([right], [place(1)])
    right_far, left_far = after(parts_right, right_far, left_far)
    far = place(2)
    right_far, left_far = score([right_far, left_far], [far[: ring // 2], far[ring // 2 :]])
    parts_left = score([left], [place(-1)])
    parts = [parts_own[0], parts_right[0], parts_left[0]]

    right, left = take(right_far, -1), take(left_far, 1)
    right, left = merge([(parts[1], 0, 0), (right, 0, 0)], [(parts[2], 0, 0), (left, ring // 2, 0)])
    right, left = after(w_theirs, right, left)
    right, left = take(right, -1), take(left, 1)
    (summed,) = merge([(parts[0], 0, 0), (right, 0, 0), (left, 0, 0)])
    own = finish(lax.all_to_all(summed, CTX, 0, 0, axis_index_groups=classes, tiled=True))
    rows = own.reshape(KVH // 2, 2 * tokens, per_group, HD).transpose(1, 0, 2, 3).reshape(2 * tokens, half)

    keep = lax.dynamic_slice_in_dim(rows, core * tokens, tokens, 0)
    other = swap(lax.dynamic_slice_in_dim(rows, (1 - core) * tokens, tokens, 0))
    attended = jnp.where(
        core == 0, jnp.concatenate([keep, other], axis=1), jnp.concatenate([other, keep], axis=1)
    )

    own, right, left, right_far, left_far, _ = gathered(rows)
    mine, other = [], []
    for chunks in ([left, own, right], [right_far, left_far]):
        lhs = jnp.concatenate(chunks).reshape(-1, half)
        other.append(jnp.dot(lhs, w_theirs, preferred_element_type=jnp.float32))
        mine.append(jnp.dot(lhs, w_mine, preferred_element_type=jnp.float32))
    out = jnp.concatenate(mine) + swap(jnp.concatenate(other))
    out = out.astype(jnp.bfloat16).reshape(HOP, ring, 2 * tokens, -1).transpose(1, 0, 2, 3)
    out = lax.dynamic_slice_in_dim(jnp.concatenate([out, out], axis=1), (1 - chip) % HOP, HOP, 1)
    return attended, out.reshape(chips * 2 * tokens, -1)


def solution(mesh):
    return jax.shard_map(
        shards,
        mesh=mesh,
        in_specs=(
            P(SPREAD, None),
            P(SPREAD, None),
            P(SPREAD, None),
            P("groups"),
            P("groups"),
            P(None, CTX),
        ),
        out_specs=(P(SPREAD, None), P("groups", CTX)),
        check_vma=False,
    )
```

profile of v0, /device:TPU:37, one launch (start us, length us, event | category | flops | bytes accessed | tf_op | source)
XLA Modules:
  0.0 279.1 jit_solution(11893964349730376982)
XLA Ops:
  0.6 20.5 %collective-permute-start = (bf16[1024,1024]{1,0:T(8,128)(2,1)}, bf16[1024,1024]{1,0:T(8,128)(2,1)}, u32[]{:S(2)}, u32[]{:S(2)}) collective-permute-start(bf16[1024,1024]{1,0:T(8,128)(2,1)} %mine_v.1), channel_id=1, source_target_pairs={{0,1},{1,0},{2,3},{3,2},{4,5},{5,4},{6,7},{7,6},{8,9},{9,8},{10,11... | collective-permute-start | bytes 6291464 | tf_op jit(solution)/shard_map/ppermute | solution.py:215
  21.2 0.7 constant_dynamic-slice_fusion.7
  21.9 0.8 dynamic-slice_bitcast_fusion
  22.7 0.0 copy-start.11
  22.7 0.0 copy-start.12
  22.7 0.2 collective-permute-start.1
  22.9 3.0 %constant_dynamic-slice_fusion.3 = bf16[4096,256]{1,0:T(8,128)(2,1)} fusion(bf16[8192,256]{1,0:T(8,128)(2,1)} %param.11, s32[]{:T(128)S(6)} %select_n.104), kind=kLoop, calls=%fused_computation.35 | loop fusion | bytes 4194308 | tf_op jit(solution)/shard_map/dynamic_slice | solution.py:259
  26.0 0.4 collective-permute-start.8
  26.4 0.1 reshape.36
  26.5 0.1 broadcast_in_dim.7
  26.6 0.1 reshape_reshape.3
  26.8 0.6 fusion.22
  27.4 0.1 fusion.21
  27.4 0.1 pad_add_fusion
  27.6 1.9 pad_add_fusion.1.lens_ref
  29.5 0.1 copy.41.pos_new
  29.6 0.0 collective-permute-done.1
  29.7 36.8 %all_gather.6.refs_0_ = bf16[8,2,128,128]{3,2,1,0:T(8,128)(2,1)S(1)} all-gather(bf16[1,2,128,128]{3,2,1,0:T(8,128)(2,1)S(1)} %bitcast.67), channel_id=1, replica_groups={{0,8,16,24,32,40,48,56},{1,9,17,25,33,41,49,57},{2,10,18,26,34,42,50,58..., dimensions={0}, use_global_device_ids=true | all-gather | bytes 589824 | tf_op jit(solution)/shard_map/all_gather | solution.py:232
  66.4 3.1 %collective-permute-start.2 = (bf16[8,2,128,128]{3,2,1,0:T(8,128)(2,1)S(1)}, bf16[8,2,128,128]{3,2,1,0:T(8,128)(2,1)S(1)}, u32[]{:S(2)}, u32[]{:S(2)}) collective-permute-start(bf16[8,2,128,128]{3,2,1,0:T(8,128)(2,1)S(1)} %all_gather.6.refs_0_), channel_id=1, source_target_pairs={{0,62},{1,63},{2,0},{3,1},{4,2},{5,3},{6,4},{7,5},{8,6},{9,7},{10,... | collective-permute-start | bytes 1572872 | tf_op jit(solution)/shard_map/ppermute | solution.py:212
  69.6 4.0 %prepare.1 = (bf16[2,2048,256]{2,1,0:T(8,128)(2,1)}, bf16[2,128,2048]{2,1,0:T(8,128)(2,1)}) custom-call(s32[3]{0:T(128)} %pad_add_fusion.1.lens_ref, bf16[1024,1024]{1,0:T(8,128)(2,1)} %mine_v.1, bf16[1024,1024]{1,0:T(8,128)(2,1)} %mine_v.1, bf16[1024,1024]{1,0:T(8,128)(2,1)} %collective-permute-done.theirs_k.theirs_v, ...), custom_call_target="tpu_custom_call" | custom-call | flops 268435456 | bytes 5242880 | tf_op jit(solution)/shard_map/prepare/pallas_call | solution.py:39
  73.6 1.6 copy-done.3
  75.2 1.2 copy-done.4
  76.4 7.4 %attend.4.refs_0_ = bf16[8,2,144,128]{3,2,1,0:T(8,128)(2,1)S(1)} custom-call(s32[16,1]{1,0:T(8,128)S(1)} %copy.41.pos_new, bf16[2,2048,256]{2,1,0:T(8,128)(2,1)S(1)} %copy-done.3, bf16[2,128,2048]{2,1,0:T(8,128)(2,1)S(1)} %copy-done.4, bf16[2,16,128]{2,1,0:T(8,128)(2,1)S(1)} %get-tuple-element.50.new_k, bf16[2,16,128]{2,1,0:T(8,128)(2,1)S(1)} %get-tuple-element.49.new_v, ...), custom_call_target="tpu_custom_call" | custom-call | flops 3221225472 | bytes 4194304 | tf_op jit(solution)/shard_map/attend/pallas_call | solution.py:122
  83.8 0.0 collective-permute-done.2.refs_0_
  83.9 2.8 %collective-permute-start.4 = (bf16[4,2,128,128]{3,2,1,0:T(8,128)(2,1)S(1)}, bf16[4,2,128,128]{3,2,1,0:T(8,128)(2,1)S(1)}, u32[]{:S(2)}, u32[]{:S(2)}) collective-permute-start(bf16[4,2,128,128]{3,2,1,0:T(8,128)(2,1)S(1)} %slice.40), channel_id=1, source_target_pairs={{0,62},{1,63},{2,0},{3,1},{4,2},{5,3},{6,4},{7,5},{8,6},{9,7},{10,... | collective-permute-start | bytes 786440 | tf_op jit(solution)/shard_map/ppermute | solution.py:212
  86.7 0.3 collective-permute-start.5
  87.0 7.5 %attend.5.refs_0_ = bf16[8,2,144,128]{3,2,1,0:T(8,128)(2,1)S(1)} custom-call(s32[16,1]{1,0:T(8,128)S(1)} %copy.41.pos_new, bf16[2,2048,256]{2,1,0:T(8,128)(2,1)S(1)} %copy-done.3, bf16[2,128,2048]{2,1,0:T(8,128)(2,1)S(1)} %copy-done.4, bf16[2,16,128]{2,1,0:T(8,128)(2,1)S(1)} %get-tuple-element.50.new_k, bf16[2,16,128]{2,1,0:T(8,128)(2,1)S(1)} %get-tuple-element.49.new_v, ...), custom_call_target="tpu_custom_call" | custom-call | flops 3221225472 | bytes 4194304 | tf_op jit(solution)/shard_map/attend/pallas_call | solution.py:122
  94.5 0.8 copy-done
  95.3 0.0 collective-permute-done.4.refs_0_
  95.3 7.2 %attend.6 = (bf16[4,2,144,128]{3,2,1,0:T(8,128)(2,1)S(1)}, bf16[4,2,144,128]{3,2,1,0:T(8,128)(2,1)S(1)}) custom-call(s32[16,1]{1,0:T(8,128)S(1)} %copy.41.pos_new, bf16[2,2048,256]{2,1,0:T(8,128)(2,1)S(1)} %copy-done.3, bf16[2,128,2048]{2,1,0:T(8,128)(2,1)S(1)} %copy-done.4, bf16[2,16,128]{2,1,0:T(8,128)(2,1)S(1)} %get-tuple-element.50.new_k, ...), custom_call_target="tpu_custom_call" | custom-call | flops 3221225472 | bytes 4194304 | tf_op jit(solution)/shard_map/attend/pallas_call | solution.py:122
  102.5 0.1 collective-permute-start.6
  102.6 2.7 collective-permute-start.7
  105.4 7.4 %attend.7.refs_2_ = bf16[8,2,144,128]{3,2,1,0:T(8,128)(2,1)S(1)} custom-call(s32[16,1]{1,0:T(8,128)S(1)} %copy.41.pos_new, bf16[2,2048,256]{2,1,0:T(8,128)(2,1)S(1)} %copy-done.3, bf16[2,128,2048]{2,1,0:T(8,128)(2,1)S(1)} %copy-done.4, bf16[2,16,128]{2,1,0:T(8,128)(2,1)S(1)} %get-tuple-element.50.new_k, bf16[2,16,128]{2,1,0:T(8,128)(2,1)S(1)} %get-tuple-element.49.new_v, ...), custom_call_target="tpu_custom_call" | custom-call | flops 3221225472 | bytes 4194304 | tf_op jit(solution)/shard_map/attend/pallas_call | solution.py:122
  112.8 0.8 copy-done.1
  113.6 0.7 copy-done.9
  114.3 0.8 copy-done.10
  115.1 3.1 %merge.2 = (bf16[8,2,144,128]{3,2,1,0:T(8,128)(2,1)}, bf16[8,2,144,128]{3,2,1,0:T(8,128)(2,1)}) custom-call(bf16[8,2,144,128]{3,2,1,0:T(8,128)(2,1)} %copy-done, bf16[4,2,144,128]{3,2,1,0:T(8,128)(2,1)} %copy-done.9, bf16[8,2,144,128]{3,2,1,0:T(8,128)(2,1)} %copy-done.1, bf16[4,2,144,128]{3,2,1,0:T(8,128)(2,1)} %copy-done.10), custom_call_target="tpu_custom_call" | custom-call | tf_op jit(solution)/shard_map/merge/pallas_call | solution.py:180
  118.2 2.7 collective-permute-start.10
  120.9 7.5 %collective-permute-done.9.refs_1_ = bf16[8,2,144,128]{3,2,1,0:T(8,128)(2,1)S(1)} collective-permute-done((bf16[8,2,144,128]{3,2,1,0:T(8,128)(2,1)}, bf16[8,2,144,128]{3,2,1,0:T(8,128)(2,1)S(1)}, u32[]{:S(2)}, u32[]{:S(2)}) %collective-permute-start.9) | collective-permute-done | bytes 589856 | tf_op jit(solution)/shard_map/ppermute | solution.py:212
  128.4 0.8 copy-done.7
  129.2 0.8 copy-done.8
  130.0 3.0 %merge.3 = bf16[8,2,144,128]{3,2,1,0:T(8,128)(2,1)} custom-call(bf16[8,2,144,128]{3,2,1,0:T(8,128)(2,1)} %copy-done.2, bf16[8,2,144,128]{3,2,1,0:T(8,128)(2,1)} %copy-done.7, bf16[8,2,144,128]{3,2,1,0:T(8,128)(2,1)} %copy-done.8), custom_call_target="tpu_custom_call" | custom-call | tf_op jit(solution)/shard_map/merge/pallas_call | solution.py:180
  133.0 10.2 %all-to-all-start = ((bf16[8,2,144,128]{3,2,1,0:T(8,128)(2,1)}), bf16[8,2,144,128]{3,2,1,0:T(8,128)(2,1)S(1)}, u32[]{:S(2)}, u32[]{:S(2)}) async-start(bf16[8,2,144,128]{3,2,1,0:T(8,128)(2,1)} %merge.3), calls=%async_computation | async-start | bytes 1179648 | tf_op jit(solution)/shard_map/all_to_all | solution.py:278
  143.2 58.8 %all-to-all-done.parts_ref = bf16[8,2,144,128]{3,2,1,0:T(8,128)(2,1)S(1)} async-done(((bf16[8,2,144,128]{3,2,1,0:T(8,128)(2,1)}), bf16[8,2,144,128]{3,2,1,0:T(8,128)(2,1)S(1)}, u32[]{:S(2)}, u32[]{:S(2)}) %all-to-all-start) | async-done | bytes 589856 | tf_op jit(solution)/shard_map/all_to_all | solution.py:278
  201.9 0.8 copy-done.6
  202.8 1.9 finish.1
  204.7 0.8 copy.63
  205.6 0.8 collective-permute-start.11
  206.4 42.2 %all_gather.7 = bf16[8,8,4096]{2,1,0:T(8,128)(2,1)S(1)} all-gather(bf16[1,8,4096]{2,1,0:T(8,128)(2,1)S(1)} %all_gather_reshape.7), channel_id=1, replica_groups={{0,8,16,24,32,40,48,56},{1,9,17,25,33,41,49,57},{2,10,18,26,34,42,50,58..., dimensions={0}, use_global_device_ids=true | all-gather | bytes 589824 | tf_op jit(solution)/shard_map/all_gather | solution.py:232
  248.6 3.0 %collective-permute-start.12 = (bf16[8,8,4096]{2,1,0:T(8,128)(2,1)S(1)}, bf16[8,8,4096]{2,1,0:T(8,128)(2,1)S(1)}, u32[]{:S(2)}, u32[]{:S(2)}) collective-permute-start(bf16[8,8,4096]{2,1,0:T(8,128)(2,1)S(1)} %all_gather.7), channel_id=1, source_target_pairs={{0,62},{1,63},{2,0},{3,1},{4,2},{5,3},{6,4},{7,5},{8,6},{9,7},{10,... | collective-permute-start | bytes 1572872 | tf_op jit(solution)/shard_map/ppermute | solution.py:212
  251.6 0.7 maximum_select_fusion.1
  252.2 7.8 %collective-permute-done.12 = bf16[8,8,4096]{2,1,0:T(8,128)(2,1)S(1)} collective-permute-done((bf16[8,8,4096]{2,1,0:T(8,128)(2,1)S(1)}, bf16[8,8,4096]{2,1,0:T(8,128)(2,1)S(1)}, u32[]{:S(2)}, u32[]{:S(2)}) %collective-permute-start.12) | collective-permute-done | bytes 524320 | tf_op jit(solution)/shard_map/ppermute | solution.py:212
  260.1 2.5 collective-permute-done.13
  262.6 0.1 collective-permute-start.15
  262.8 2.8 collective-permute-start.14
  265.6 2.3 fusion.4
  267.9 1.3 collective-permute-done.15
  269.2 2.1 fusion.5
  271.3 5.8 %collective-permute-start.16 = (f32[256,256]{1,0:T(8,128)S(1)}, f32[256,256]{1,0:T(8,128)S(1)}, u32[]{:S(2)}, u32[]{:S(2)}) collective-permute-start(f32[256,256]{1,0:T(8,128)S(1)} %pad_maximum_fusion), channel_id=1, source_target_pairs={{0,1},{1,0},{2,3},{3,2},{4,5},{5,4},{6,7},{7,6},{8,9},{9,8},{10,11... | collective-permute-start | bytes 786440 | tf_op jit(solution)/shard_map/ppermute | solution.py:215
  277.1 0.6 fusion.2
  277.7 0.5 fusion
  278.2 0.1 collective-permute-done.16
  278.3 0.1 fusion.7
  278.4 0.7 copy.48
  (50 shorter events, 0.4 us)
Async XLA Ops:
  0.6 68.9 %collective-permute-start = (bf16[1024,1024]{1,0:T(8,128)(2,1)}, bf16[1024,1024]{1,0:T(8,128)(2,1)}, u32[]{:S(2)}, u32[]{:S(2)}) collective-permute-start(bf16[1024,1024]{1,0:T(8,128)(2,1)} %mine_v.1), channel_id=1, source_target_pairs={{0,1},{1,0},{2,3},{3,2},{4,5},{5,4},{6,7},{7,6},{8,9},{9,8},{10,11... | collective-permute-start | bytes 6291464 | tf_op jit(solution)/shard_map/ppermute | solution.py:215
  22.7 3.7 %copy-start.11 = (s32[256]{0:T(256)S(1)}, s32[256]{0:T(256)}, u32[]{:S(2)}) copy-start(s32[256]{0:T(256)} %param.9) | copy-start | bytes 3076
  22.7 4.0 %copy-start.12 = (s32[64]{0:T(128)S(1)}, s32[64]{0:T(128)}, u32[]{:S(2)}) copy-start(s32[64]{0:T(128)} %param.10) | copy-start | bytes 772
  22.7 6.9 %collective-permute-start.1 = (bf16[4,4608]{1,0:T(4,128)(2,1)S(1)}, bf16[4,4608]{1,0:T(4,128)(2,1)S(1)}, u32[]{:S(2)}, u32[]{:S(2)}) collective-permute-start(bf16[4,4608]{1,0:T(4,128)(2,1)S(1)} %pad_maximum_fusion.1), channel_id=1, source_target_pairs={{0,1},{1,0},{2,3},{3,2},{4,5},{5,4},{6,7},{7,6},{8,9},{9,8},{10,11... | collective-permute-start | bytes 110600 | tf_op jit(solution)/shard_map/ppermute | solution.py:215
  26.0 92.2 %collective-permute-start.8 = (bf16[4096,256]{1,0:T(8,128)(2,1)}, bf16[4096,256]{1,0:T(8,128)(2,1)}, u32[]{:S(2)}, u32[]{:S(2)}) collective-permute-start(bf16[4096,256]{1,0:T(8,128)(2,1)} %constant_dynamic-slice_fusion.3), channel_id=1, source_target_pairs={{0,1},{1,0},{2,3},{3,2},{4,5},{5,4},{6,7},{7,6},{8,9},{9,8},{10,11... | collective-permute-start | bytes 6291464 | tf_op jit(solution)/shard_map/ppermute | solution.py:215
  66.4 17.4 %collective-permute-start.2 = (bf16[8,2,128,128]{3,2,1,0:T(8,128)(2,1)S(1)}, bf16[8,2,128,128]{3,2,1,0:T(8,128)(2,1)S(1)}, u32[]{:S(2)}, u32[]{:S(2)}) collective-permute-start(bf16[8,2,128,128]{3,2,1,0:T(8,128)(2,1)S(1)} %all_gather.6.refs_0_), channel_id=1, source_target_pairs={{0,62},{1,63},{2,0},{3,1},{4,2},{5,3},{6,4},{7,5},{8,6},{9,7},{10,... | collective-permute-start | bytes 1572872 | tf_op jit(solution)/shard_map/ppermute | solution.py:212
  69.5 14.4 %collective-permute-start.3 = (bf16[8,2,128,128]{3,2,1,0:T(8,128)(2,1)S(1)}, bf16[8,2,128,128]{3,2,1,0:T(8,128)(2,1)S(1)}, u32[]{:S(2)}, u32[]{:S(2)}) collective-permute-start(bf16[8,2,128,128]{3,2,1,0:T(8,128)(2,1)S(1)} %all_gather.6.refs_0_), channel_id=1, source_target_pairs={{0,2},{1,3},{2,4},{3,5},{4,6},{5,7},{6,8},{7,9},{8,10},{9,11},{10,... | collective-permute-start | bytes 1572872 | tf_op jit(solution)/shard_map/ppermute | solution.py:212
  73.6 1.6 copy-start.3
  75.1 1.2 copy-start.4
  83.8 3.2 %copy-start.2 = (bf16[8,2,144,128]{3,2,1,0:T(8,128)(2,1)}, bf16[8,2,144,128]{3,2,1,0:T(8,128)(2,1)S(1)}, u32[]{:S(2)}) copy-start(bf16[8,2,144,128]{3,2,1,0:T(8,128)(2,1)S(1)} %attend.4.refs_0_) | copy-start | bytes 1769476
  83.9 11.4 %collective-permute-start.4 = (bf16[4,2,128,128]{3,2,1,0:T(8,128)(2,1)S(1)}, bf16[4,2,128,128]{3,2,1,0:T(8,128)(2,1)S(1)}, u32[]{:S(2)}, u32[]{:S(2)}) collective-permute-start(bf16[4,2,128,128]{3,2,1,0:T(8,128)(2,1)S(1)} %slice.40), channel_id=1, source_target_pairs={{0,62},{1,63},{2,0},{3,1},{4,2},{5,3},{6,4},{7,5},{8,6},{9,7},{10,... | collective-permute-start | bytes 786440 | tf_op jit(solution)/shard_map/ppermute | solution.py:212
  86.7 8.6 %collective-permute-start.5 = (bf16[4,2,128,128]{3,2,1,0:T(8,128)(2,1)S(1)}, bf16[4,2,128,128]{3,2,1,0:T(8,128)(2,1)S(1)}, u32[]{:S(2)}, u32[]{:S(2)}) collective-permute-start(bf16[4,2,128,128]{3,2,1,0:T(8,128)(2,1)S(1)} %slice.41), channel_id=1, source_target_pairs={{0,2},{1,3},{2,4},{3,5},{4,6},{5,7},{6,8},{7,9},{8,10},{9,11},{10,... | collective-permute-start | bytes 786440 | tf_op jit(solution)/shard_map/ppermute | solution.py:212
  94.5 0.8 copy-start
  102.5 11.1 %collective-permute-start.6 = (bf16[4,2,144,128]{3,2,1,0:T(8,128)(2,1)S(1)}, bf16[4,2,144,128]{3,2,1,0:T(8,128)(2,1)S(1)}, u32[]{:S(2)}, u32[]{:S(2)}) collective-permute-start(bf16[4,2,144,128]{3,2,1,0:T(8,128)(2,1)S(1)} %get-tuple-element.22), channel_id=1, source_target_pairs={{0,2},{1,3},{2,4},{3,5},{4,6},{5,7},{6,8},{7,9},{8,10},{9,11},{10,... | collective-permute-start | bytes 884744 | tf_op jit(solution)/shard_map/ppermute | solution.py:212
  102.6 11.0 %collective-permute-start.7 = (bf16[4,2,144,128]{3,2,1,0:T(8,128)(2,1)S(1)}, bf16[4,2,144,128]{3,2,1,0:T(8,128)(2,1)S(1)}, u32[]{:S(2)}, u32[]{:S(2)}) collective-permute-start(bf16[4,2,144,128]{3,2,1,0:T(8,128)(2,1)S(1)} %get-tuple-element.23), channel_id=1, source_target_pairs={{0,62},{1,63},{2,0},{3,1},{4,2},{5,3},{6,4},{7,5},{8,6},{9,7},{10,... | collective-permute-start | bytes 884744 | tf_op jit(solution)/shard_map/ppermute | solution.py:212
  112.8 0.8 copy-start.1
  113.6 0.7 copy-start.9
  114.3 0.8 copy-start.10
  118.2 10.2 %collective-permute-start.9 = (bf16[8,2,144,128]{3,2,1,0:T(8,128)(2,1)}, bf16[8,2,144,128]{3,2,1,0:T(8,128)(2,1)S(1)}, u32[]{:S(2)}, u32[]{:S(2)}) collective-permute-start(bf16[8,2,144,128]{3,2,1,0:T(8,128)(2,1)} %get-tuple-element.26), channel_id=1, source_target_pairs={{0,2},{1,3},{2,4},{3,5},{4,6},{5,7},{6,8},{7,9},{8,10},{9,11},{10,... | collective-permute-start | bytes 1769480 | tf_op jit(solution)/shard_map/ppermute | solution.py:212
  118.2 10.2 %collective-permute-start.10 = (bf16[8,2,144,128]{3,2,1,0:T(8,128)(2,1)}, bf16[8,2,144,128]{3,2,1,0:T(8,128)(2,1)S(1)}, u32[]{:S(2)}, u32[]{:S(2)}) collective-permute-start(bf16[8,2,144,128]{3,2,1,0:T(8,128)(2,1)} %get-tuple-element.27), channel_id=1, source_target_pairs={{0,62},{1,63},{2,0},{3,1},{4,2},{5,3},{6,4},{7,5},{8,6},{9,7},{10,... | collective-permute-start | bytes 1769480 | tf_op jit(solution)/shard_map/ppermute | solution.py:212
  128.3 0.8 copy-start.7
  129.2 0.8 copy-start.8
  133.0 68.9 %all-to-all-start = ((bf16[8,2,144,128]{3,2,1,0:T(8,128)(2,1)}), bf16[8,2,144,128]{3,2,1,0:T(8,128)(2,1)S(1)}, u32[]{:S(2)}, u32[]{:S(2)}) async-start(bf16[8,2,144,128]{3,2,1,0:T(8,128)(2,1)} %merge.3), calls=%async_computation | async-start | bytes 1179648 | tf_op jit(solution)/shard_map/all_to_all | solution.py:278
  201.9 0.8 copy-start.6
  205.6 46.0 %collective-permute-start.11 = (bf16[4,4096]{1,0:T(4,128)(2,1)S(1)}, bf16[4,4096]{1,0:T(4,128)(2,1)S(1)}, u32[]{:S(2)}, u32[]{:S(2)}) collective-permute-start(bf16[4,4096]{1,0:T(4,128)(2,1)S(1)} %get-tuple-element.33), channel_id=1, source_target_pairs={{0,1},{1,0},{2,3},{3,2},{4,5},{5,4},{6,7},{7,6},{8,9},{9,8},{10,11... | collective-permute-start | bytes 98312 | tf_op jit(solution)/shard_map/ppermute | solution.py:215
  248.6 11.5 %collective-permute-start.12 = (bf16[8,8,4096]{2,1,0:T(8,128)(2,1)S(1)}, bf16[8,8,4096]{2,1,0:T(8,128)(2,1)S(1)}, u32[]{:S(2)}, u32[]{:S(2)}) collective-permute-start(bf16[8,8,4096]{2,1,0:T(8,128)(2,1)S(1)} %all_gather.7), channel_id=1, source_target_pairs={{0,62},{1,63},{2,0},{3,1},{4,2},{5,3},{6,4},{7,5},{8,6},{9,7},{10,... | collective-permute-start | bytes 1572872 | tf_op jit(solution)/shard_map/ppermute | solution.py:212
  251.6 11.0 %collective-permute-start.13 = (bf16[8,8,4096]{2,1,0:T(8,128)(2,1)S(1)}, bf16[8,8,4096]{2,1,0:T(8,128)(2,1)S(1)}, u32[]{:S(2)}, u32[]{:S(2)}) collective-permute-start(bf16[8,8,4096]{2,1,0:T(8,128)(2,1)S(1)} %all_gather.7), channel_id=1, source_target_pairs={{0,2},{1,3},{2,4},{3,5},{4,6},{5,7},{6,8},{7,9},{8,10},{9,11},{10,... | collective-permute-start | bytes 1572872 | tf_op jit(solution)/shard_map/ppermute | solution.py:212
  262.6 6.6 %collective-permute-start.15 = (bf16[4,8,4096]{2,1,0:T(8,128)(2,1)S(1)}, bf16[4,8,4096]{2,1,0:T(8,128)(2,1)S(1)}, u32[]{:S(2)}, u32[]{:S(2)}) collective-permute-start(bf16[4,8,4096]{2,1,0:T(8,128)(2,1)S(1)} %slice.47), channel_id=1, source_target_pairs={{0,2},{1,3},{2,4},{3,5},{4,6},{5,7},{6,8},{7,9},{8,10},{9,11},{10,... | collective-permute-start | bytes 786440 | tf_op jit(solution)/shard_map/ppermute | solution.py:212
  262.8 6.4 %collective-permute-start.14 = (bf16[4,8,4096]{2,1,0:T(8,128)(2,1)S(1)}, bf16[4,8,4096]{2,1,0:T(8,128)(2,1)S(1)}, u32[]{:S(2)}, u32[]{:S(2)}) collective-permute-start(bf16[4,8,4096]{2,1,0:T(8,128)(2,1)S(1)} %slice.46), channel_id=1, source_target_pairs={{0,62},{1,63},{2,0},{3,1},{4,2},{5,3},{6,4},{7,5},{8,6},{9,7},{10,... | collective-permute-start | bytes 786440 | tf_op jit(solution)/shard_map/ppermute | solution.py:212
  265.6 11.6 %copy-start.5 = (bf16[8192,256]{1,0:T(8,128)(2,1)S(1)}, bf16[8192,256]{1,0:T(8,128)(2,1)}, u32[]{:S(2)}) copy-start(bf16[8192,256]{1,0:T(8,128)(2,1)} %param.11) | copy-start | bytes 12582916
  271.3 6.9 %collective-permute-start.16 = (f32[256,256]{1,0:T(8,128)S(1)}, f32[256,256]{1,0:T(8,128)S(1)}, u32[]{:S(2)}, u32[]{:S(2)}) collective-permute-start(f32[256,256]{1,0:T(8,128)S(1)} %pad_maximum_fusion), channel_id=1, source_target_pairs={{0,1},{1,0},{2,3},{3,2},{4,5},{5,4},{6,7},{7,6},{8,9},{9,8},{10,11... | collective-permute-start | bytes 786440 | tf_op jit(solution)/shard_map/ppermute | solution.py:215
where the time goes:
time: 281 us; the launch traced here: 279 us
  blocking collectives  79 us (28%)
  waiting for transfers between devices  78.1 us (28%)
  starting transfers between devices  55.4 us (20%)
  Pallas kernels  41.4 us (15%)
  local copies, waits for them, and re-layouts  15.8 us (6%)
  matrix products  5.46 us (2%)
  other arithmetic  2.85 us (1%)
    all_gather x2, blocking collectives, gathered(): own = lax.all_gather(block, CTX, axis_index_groups=classes)  79 us
    all_to_all x1, waiting for transfers between devices, shards(): lax.all_to_all(summed, CTX, 0, 0, axis_index_groups=classes, tiled=True)  58.8 us
    pallas_call x4, Pallas kernels, attend(): pl.pallas_call(attend_body, grid=(KVH // 2,), in_specs=[whole(pos_new), p...  29.5 us
    ppermute x5, starting transfers between devices, swap(): return lax.ppermute(x, CTX, [(i, i ^ 1) for i in range(devices)])  27.7 us
    ppermute x12, waiting for transfers between devices, take(): lax.ppermute(x, CTX, [(i, (i - 2 * d) % devices) for i in range(devices)])  19.2 us
    ppermute x12, starting transfers between devices, take(): lax.ppermute(x, CTX, [(i, (i - 2 * d) % devices) for i in range(devices)])  17.6 us
    all_to_all x1, starting transfers between devices, shards(): lax.all_to_all(summed, CTX, 0, 0, axis_index_groups=classes, tiled=True)  10.2 us
    unnamed x31, local copies, waits for them, and re-layouts  9.25 us
  transfers between devices with their start and end apart: 18, of which 6 were waited for; matrix products, arithmetic and copies ran while one was open for 4% of the time, Pallas kernels for 13%

commit v1 on v0

--- a/solution.py
+++ b/solution.py
@@ -14,7 +14,7 @@
 CTX = "ctx"
 SPREAD = ("groups", "ctx")
 TILE = 4
-HOP = 4
+HOP = 8
 TAIL = 16
 ROWS = HD + TAIL
 DEAD = -1e30
@@ -71,6 +71,7 @@
 
 
 def attend_body(pos_new, keys_ref, values_ref, new_k, new_v, *refs):
+    *refs, all_q, all_pos, all_out = refs
     count = len(refs) // 3
     nt = (((1,), (1,)), ((), ()))
     tn = (((0,), (0,)), ((), ()))
@@ -80,37 +81,47 @@
         p = jnp.exp2((s - top) * TO_LOG2)
         return top, jnp.sum(p, axis=0, keepdims=True), p.astype(jnp.bfloat16)
 
-    for q_ref, pos_ref, out_ref in zip(refs[:count], refs[count : 2 * count], refs[2 * count :]):
-
-        def tile(i, carry, q_ref=q_ref, pos_ref=pos_ref, out_ref=out_ref):
-            base = i * TILE
-            q = jnp.concatenate([q_ref[base + k, 0] for k in range(TILE)], axis=0)
-            at = jnp.concatenate([pos_ref[base + k] for k in range(TILE)], axis=1)
-            lane = lax.broadcasted_iota(jnp.int32, q.shape, 1)
-            q_wide = jnp.concatenate([q, jnp.where(lane == 0, 1.0, 0.0).astype(q.dtype)], axis=1)
-            s = lax.dot_general(keys_ref[0], q_wide, nt, preferred_element_type=jnp.float32)
-            top_a, total_a, p = softmax(s)
-            out_a = jnp.dot(values_ref[0], p, preferred_element_type=jnp.float32)
-            s = lax.dot_general(new_k[0], q, nt, preferred_element_type=jnp.float32)
-            top_b, total_b, p = softmax(jnp.where(at >= pos_new[...], s, DEAD))
-            out_b = lax.dot_general(new_v[0], p, tn, preferred_element_type=jnp.float32)
-            best = jnp.maximum(top_a, top_b)
-            keep_a = jnp.exp2((top_a - best) * TO_LOG2)
-            keep_b = jnp.exp2((top_b - best) * TO_LOG2)
-            total = keep_a * total_a + keep_b * total_b
-            out = (keep_a * out_a + keep_b * out_b) * (1.0 / total)
-            out = out.astype(jnp.bfloat16)
-            tail = tail_rows(best * TO_LOG2 + jnp.log2(total))
-            for k in range(TILE):
-                lanes = slice(k * HD, (k + 1) * HD)
-                out_ref[base + k, 0, :HD, :] = out[:, lanes]
-                out_ref[base + k, 0, HD:, :] = tail[:, lanes]
-            return carry
-
-        if q_ref.shape[0] == TILE:
-            tile(0, 0)
-        else:
-            lax.fori_loop(0, q_ref.shape[0] // TILE, tile, 0)
+    place = 0
+    for q_ref, pos_ref in zip(refs[:count], refs[count : 2 * count]):
+        for k in range(q_ref.shape[0]):
+            all_q[place + k] = q_ref[k, 0]
+            all_pos[place + k] = pos_ref[k]
+        place += q_ref.shape[0]
+
+    def tile(i, carry):
+        base = i * TILE
+        q = jnp.concatenate([all_q[base + k] for k in range(TILE)], axis=0)
+        at = jnp.concatenate([all_pos[base + k] for k in range(TILE)], axis=1)
+        lane = lax.broadcasted_iota(jnp.int32, q.shape, 1)
+        q_wide = jnp.concatenate([q, jnp.where(lane == 0, 1.0, 0.0).astype(q.dtype)], axis=1)
+        s = lax.dot_general(keys_ref[0], q_wide, nt, preferred_element_type=jnp.float32)
+        top_a, total_a, p = softmax(s)
+        out_a = jnp.dot(values_ref[0], p, preferred_element_type=jnp.float32)
+        s = lax.dot_general(new_k[0], q, nt, preferred_element_type=jnp.float32)
+        top_b, total_b, p = softmax(jnp.where(at >= pos_new[...], s, DEAD))
+        out_b = lax.dot_general(new_v[0], p, tn, preferred_element_type=jnp.float32)
+        best = jnp.maximum(top_a, top_b)
+        keep_a = jnp.exp2((top_a - best) * TO_LOG2)
+        keep_b = jnp.exp2((top_b - best) * TO_LOG2)
+        total = keep_a * total_a + keep_b * total_b
+        out = (keep_a * out_a + keep_b * out_b) * (1.0 / total)
+        out = out.astype(jnp.bfloat16)
+        tail = tail_rows(best * TO_LOG2 + jnp.log2(total))
+        for k in range(TILE):
+            lanes = slice(k * HD, (k + 1) * HD)
+            all_out[base + k, :HD, :] = out[:, lanes]
+            all_out[base + k, HD:, :] = tail[:, lanes]
+        return carry
+
+    if place == TILE:
+        tile(0, 0)
+    else:
+        lax.fori_loop(0, place // TILE, tile, 0)
+    place = 0
+    for out_ref in refs[2 * count :]:
+        for k in range(out_ref.shape[0]):
+            out_ref[k, 0] = all_out[place + k]
+        place += out_ref.shape[0]
 
 
 def attend(prepared, pos_new, new_k, new_v, blocks, places):
@@ -118,7 +129,8 @@
     per_group = lambda a: pl.BlockSpec((1, *a.shape[1:]), lambda g: (g, 0, 0))
     whole = lambda a: pl.BlockSpec(a.shape, lambda g: (0,) * a.ndim)
     one = lambda a, rows: pl.BlockSpec((a.shape[0], 1, rows, HD), lambda g: (0, g, 0, 0))
-    score_count = sum(b.shape[0] for b in blocks) * HD * keys.shape[0] * keys.shape[1]
+    count = sum(b.shape[0] for b in blocks)
+    score_count = count * HD * keys.shape[0] * keys.shape[1]
     return pl.pallas_call(
         attend_body,
         grid=(KVH // 2,),
@@ -127,6 +139,11 @@
         + [whole(p) for p in places],
         out_specs=[one(b, ROWS) for b in blocks],
         out_shape=[jax.ShapeDtypeStruct((b.shape[0], KVH // 2, ROWS, HD), jnp.bfloat16) for b in blocks],
+        scratch_shapes=[
+            pltpu.VMEM((count, HD, HD), jnp.bfloat16),
+            pltpu.VMEM((count, 1, HD), jnp.int32),
+            pltpu.VMEM((count, ROWS, HD), jnp.bfloat16),
+        ],
         compiler_params=pltpu.CompilerParams(vmem_limit_bytes=48 * 1024 * 1024),
         cost_estimate=pl.CostEstimate(
             flops=score_count * 6 * HD,
@@ -184,24 +201,26 @@
     )(*arrays)
 
 
-def finish_body(parts_ref, out_ref):
+def finish_body(*refs):
+    out_ref = refs[-1]
     for g in range(out_ref.shape[0]):
-        out, _ = merged([(parts_ref[k, g, :HD, :], parts_ref[k, g, HD:, :]) for k in range(parts_ref.shape[0])])
+        out, _ = merged([(r[0, g, :HD, :], r[0, g, HD:, :]) for r in refs[:-1]])
         out_ref[g] = out.T.astype(jnp.bfloat16)
 
 
-def finish(parts):
+def finish(*arrays):
     return pl.pallas_call(
         finish_body,
         out_shape=jax.ShapeDtypeStruct((KVH // 2, HD, HD), jnp.bfloat16),
         name="finish",
-    )(parts)
+    )(*arrays)
 
 
 def shards(queries, new_kv, prefix_cache, positions, lengths, out_weight):
     devices = lax.axis_size(CTX)
     chips = devices // 2
     ring = chips // HOP
+    reach = HOP // 2
     index = lax.axis_index(CTX)
     chip, core = index // 2, index % 2
     tokens = queries.shape[0]
@@ -228,12 +247,15 @@
 
     classes = [[2 * (b + HOP * a) + c for a in range(ring)] for b in range(HOP) for c in range(2)]
 
-    def gathered(block, last=lambda own: ()):
+    def gathered(block, fill=lambda s, chunks: ()):
         own = lax.all_gather(block, CTX, axis_index_groups=classes)
-        right, left = take(own, 1), take(own, -1)
-        done = last(own)
-        right, left = after(done, right, left)
-        return own, right, left, take(right[: ring // 2], 1), take(left[ring // 2 :], -1), done
+        chunks = [(own, own)]
+        for s in range(1, reach + 1):
+            right, left = chunks[-1]
+            if s == reach:
+                right, left = right[: ring // 2], left[ring // 2 :]
+            chunks.append(after(fill(s, chunks), take(right, 1), take(left, -1)))
+        return chunks
 
     q_mine, q_send = halves(queries, 1)
     n_mine, n_send = halves(new_kv, 1)
@@ -256,26 +278,39 @@
     prepared = prepare(core_lens, prefix_cache, theirs)
     w_mine = lax.dynamic_slice_in_dim(out_weight, core * half, half, 0)
 
-    w_send = lax.dynamic_slice_in_dim(out_weight, (1 - core) * half, half, 0)
-    w_theirs = swap(w_send)
-
     def score(blocks, places):
         return attend(prepared, pos_new, new_k, new_v, blocks, places)
 
-    own, right, left, right_far, left_far, parts_own = gathered(q_block, lambda own: score([own], [place(0)]))
-    parts_right = score([right], [place(1)])
-    right_far, left_far = after(parts_right, right_far, left_far)
-    far = place(2)
-    right_far, left_far = score([right_far, left_far], [far[: ring // 2], far[ring // 2 :]])
-    parts_left = score([left], [place(-1)])
-    parts = [parts_own[0], parts_right[0], parts_left[0]]
-
-    right, left = take(right_far, -1), take(left_far, 1)
-    right, left = merge([(parts[1], 0, 0), (right, 0, 0)], [(parts[2], 0, 0), (left, ring // 2, 0)])
-    right, left = after(w_theirs, right, left)
+    (weight,) = after(prepared, out_weight)
+    w_send = lax.dynamic_slice_in_dim(weight, (1 - core) * half, half, 0)
+    parts = {}
+
+    def fill(s, chunks):
+        if s == 1:
+            return prepared, w_send
+        k = s - 2
+        if k == 0:
+            parts[0] = score([chunks[0][0]], [place(0)])
+        else:
+            parts[k] = score(list(chunks[k]), [place(k), place(-k)])
+        return parts[k]
+
+    chunks = gathered(q_block, fill)
+    far = place(reach)
+    right, left = score(list(chunks[reach]), [far[: ring // 2], far[ring // 2 :]])
     right, left = take(right, -1), take(left, 1)
-    (summed,) = merge([(parts[0], 0, 0), (right, 0, 0), (left, 0, 0)])
-    own = finish(lax.all_to_all(summed, CTX, 0, 0, axis_index_groups=classes, tiled=True))
+    fill(reach + 1, chunks)
+    for s in range(reach - 1, 0, -1):
+        start = ring // 2 if s == reach - 1 else 0
+        right, left = merge([(parts[s][0], 0, 0), (right, 0, 0)], [(parts[s][1], 0, 0), (left, start, 0)])
+        right, left = take(right, -1), take(left, 1)
+    w_theirs = swap(w_send)
+    (summed,) = merge([(parts[0][0], 0, 0), (right, 0, 0), (left, 0, 0)])
+    (summed,) = after(w_theirs, summed)
+    piece = lambda d: lax.dynamic_slice_in_dim(summed, (chip // HOP + d) % ring, 1, 0)
+    own = finish(
+        piece(0), take(piece(1), -HOP), take(piece(ring - 1), HOP), take(piece(2), -2 * HOP)
+    )
     rows = own.reshape(KVH // 2, 2 * tokens, per_group, HD).transpose(1, 0, 2, 3).reshape(2 * tokens, half)
 
     keep = lax.dynamic_slice_in_dim(rows, core * tokens, tokens, 0)
@@ -284,15 +319,16 @@
         core == 0, jnp.concatenate([keep, other], axis=1), jnp.concatenate([other, keep], axis=1)
     )
 
-    own, right, left, right_far, left_far, _ = gathered(rows)
+    chunks = gathered(rows)
+    near = [c[1] for c in chunks[reach - 1 : 0 : -1]] + [c[0] for c in chunks[:reach]]
     mine, other = [], []
-    for chunks in ([left, own, right], [right_far, left_far]):
-        lhs = jnp.concatenate(chunks).reshape(-1, half)
+    for group in (near, chunks[reach]):
+        lhs = jnp.concatenate(group).reshape(-1, half)
         other.append(jnp.dot(lhs, w_theirs, preferred_element_type=jnp.float32))
         mine.append(jnp.dot(lhs, w_mine, preferred_element_type=jnp.float32))
     out = jnp.concatenate(mine) + swap(jnp.concatenate(other))
     out = out.astype(jnp.bfloat16).reshape(HOP, ring, 2 * tokens, -1).transpose(1, 0, 2, 3)
-    out = lax.dynamic_slice_in_dim(jnp.concatenate([out, out], axis=1), (1 - chip) % HOP, HOP, 1)
+    out = lax.dynamic_slice_in_dim(jnp.concatenate([out, out], axis=1), (reach - 1 - chip) % HOP, HOP, 1)
     return attended, out.reshape(chips * 2 * tokens, -1)
 
 

time: 281 us -> 298 us (1.060); the launches traced: 279 us -> 293 us
  starting transfers between devices: 55.4 us -> 111 us
  waiting for transfers between devices: 78.1 us -> 47.2 us
  blocking collectives: 79 us -> 57.7 us
  local copies, waits for them, and re-layouts: 15.8 us -> 24.6 us
  Pallas kernels: 41.4 us -> 45.6 us
  matrix products: 5.46 us -> 2.21 us
    all_to_all x1 -> x0, waiting for transfers between devices: 58.8 us -> none  [shards(): lax.all_to_all(summed, CTX, 0, 0, axis_index_groups=classes, tiled=True)]
    ppermute x12 -> x27, starting transfers between devices: 17.6 us -> 65.6 us  [take(): lax.ppermute(x, CTX, [(i, (i - 2 * d) % devices) for i in range(devices)])]
    ppermute x12 -> x27, waiting for transfers between devices: 19.2 us -> 47.1 us  [take(): lax.ppermute(x, CTX, [(i, (i - 2 * d) % devices) for i in range(devices)])]
    all_gather x2, blocking collectives: 79 us -> 57.7 us  [gathered(): own = lax.all_gather(block, CTX, axis_index_groups=classes)]
    ppermute x5, starting transfers between devices: 27.7 us -> 45.5 us  [swap(): return lax.ppermute(x, CTX, [(i, i ^ 1) for i in range(devices)])]
    all_to_all x1 -> x0, starting transfers between devices: 10.2 us -> none  [shards(): lax.all_to_all(summed, CTX, 0, 0, axis_index_groups=classes, tiled=True)]
    unnamed x31 -> x55, local copies, waits for them, and re-layouts: 9.25 us -> 14.1 us
    pallas_call x2 -> x4, Pallas kernels: 6.1 us -> 9.76 us  [merge(): pl.pallas_call(functools.partial(merge_body, starts), out_shape=[jax.Shap...]
  transfers between devices with their start and end apart: 18 -> 32, of which waited for: 6 -> 12; matrix products, arithmetic and copies ran while one was open for 4% -> 5% of each run, Pallas kernels for 13% -> 15%
where the time goes in v1:
time: 298 us; the launch traced here: 293 us
  starting transfers between devices  111 us (37%)
  blocking collectives  57.7 us (19%)
  waiting for transfers between devices  47.2 us (16%)
  Pallas kernels  45.6 us (15%)
  local copies, waits for them, and re-layouts  24.6 us (8%)
    ppermute x27, starting transfers between devices, take(): lax.ppermute(x, CTX, [(i, (i - 2 * d) % devices) for i in range(devices)])  65.6 us
    all_gather x2, blocking collectives, gathered(): own = lax.all_gather(block, CTX, axis_index_groups=classes)  57.7 us
    ppermute x27, waiting for transfers between devices, take(): lax.ppermute(x, CTX, [(i, (i - 2 * d) % devices) for i in range(devices)])  47.1 us
    ppermute x5, starting transfers between devices, swap(): return lax.ppermute(x, CTX, [(i, i ^ 1) for i in range(devices)])  45.5 us
    pallas_call x5, Pallas kernels, attend(): pl.pallas_call(attend_body, grid=(KVH // 2,), in_specs=[whole(pos_new), p...  30.2 us
    unnamed x55, local copies, waits for them, and re-layouts  14.1 us
    pallas_call x4, Pallas kernels, merge(): pl.pallas_call(functools.partial(merge_body, starts), out_shape=[jax.Shap...  9.76 us
  transfers between devices with their start and end apart: 32, of which 12 were waited for; matrix products, arithmetic and copies ran while one was open for 5% of the time, Pallas kernels for 15%

profile of v1, /device:TPU:37, one launch (start us, length us, event | category | flops | bytes accessed | tf_op | source)
XLA Modules:
  0.0 292.7 jit_solution(5944167032603810447)
XLA Ops:
  0.6 20.5 %collective-permute-start = (bf16[1024,1024]{1,0:T(8,128)(2,1)}, bf16[1024,1024]{1,0:T(8,128)(2,1)S(1)}, u32[]{:S(2)}, u32[]{:S(2)}) collective-permute-start(bf16[1024,1024]{1,0:T(8,128)(2,1)} %mine_v.1), channel_id=1, source_target_pairs={{0,1},{1,0},{2,3},{3,2},{4,5},{5,4},{6,7},{7,6},{8,9},{9,8},{10,11... | collective-permute-start | bytes 6291464 | tf_op jit(solution)/shard_map/ppermute | solution.py:234
  21.2 0.8 dynamic-slice_bitcast_fusion
  22.0 0.7 constant_dynamic-slice_fusion.18
  23.0 0.8 reshape.36
  24.1 1.3 fusion.29
  25.4 0.8 fusion.28
  26.3 1.9 pad_add_fusion.1.lens_ref
  28.4 28.1 %all_gather.6.refs_0_ = bf16[4,2,128,128]{3,2,1,0:T(8,128)(2,1)S(1)} all-gather(bf16[1,2,128,128]{3,2,1,0:T(8,128)(2,1)S(1)} %bitcast.76), channel_id=1, replica_groups={{0,16,32,48},{1,17,33,49},{2,18,34,50},{3,19,35,51},{4,20,36,52},{5,21,..., dimensions={0}, use_global_device_ids=true | all-gather | bytes 327680 | tf_op jit(solution)/shard_map/all_gather | solution.py:251
  56.5 5.7 %collective-permute-start.2 = (bf16[4,2,128,128]{3,2,1,0:T(8,128)(2,1)S(1)}, bf16[4,2,128,128]{3,2,1,0:T(8,128)(2,1)S(1)}, u32[]{:S(2)}, u32[]{:S(2)}) collective-permute-start(bf16[4,2,128,128]{3,2,1,0:T(8,128)(2,1)S(1)} %all_gather.6.refs_0_), channel_id=1, source_target_pairs={{0,62},{1,63},{2,0},{3,1},{4,2},{5,3},{6,4},{7,5},{8,6},{9,7},{10,... | collective-permute-start | bytes 786440 | tf_op jit(solution)/shard_map/ppermute | solution.py:231
  62.3 1.3 copy-done.10
  63.6 3.8 %prepare.1 = (bf16[2,2048,256]{2,1,0:T(8,128)(2,1)}, bf16[2,128,2048]{2,1,0:T(8,128)(2,1)}) custom-call(s32[3]{0:T(128)} %pad_add_fusion.1.lens_ref, bf16[1024,1024]{1,0:T(8,128)(2,1)} %mine_v.1, bf16[1024,1024]{1,0:T(8,128)(2,1)} %mine_v.1, bf16[1024,1024]{1,0:T(8,128)(2,1)} %copy-done.10, bf16[1024,1024]{1,0:T(8,128)(2,1)} %copy-done.10), custom_call_target="tpu_custom_call" | custom-call | flops 268435456 | bytes 5242880 | tf_op jit(solution)/shard_map/prepare/pallas_call | solution.py:39
  67.5 3.2 %constant_dynamic-slice_fusion.14 = bf16[4096,256]{1,0:T(8,128)(2,1)} fusion(bf16[8192,256]{1,0:T(8,128)(2,1)} %param.11, s32[]{:T(128)S(6)} %select_n.166), kind=kLoop, calls=%fused_computation.51 | loop fusion | bytes 4194308 | tf_op jit(solution)/shard_map/dynamic_slice | solution.py:285
  70.7 5.9 %collective-permute-start.18 = (bf16[4096,256]{1,0:T(8,128)(2,1)}, bf16[4096,256]{1,0:T(8,128)(2,1)S(1)}, u32[]{:S(2)}, u32[]{:S(2)}) collective-permute-start(bf16[4096,256]{1,0:T(8,128)(2,1)} %constant_dynamic-slice_fusion.14), channel_id=1, source_target_pairs={{0,1},{1,0},{2,3},{3,2},{4,5},{5,4},{6,7},{7,6},{8,9},{9,8},{10,11... | collective-permute-start | bytes 6291464 | tf_op jit(solution)/shard_map/ppermute | solution.py:234
  76.6 2.9 %collective-permute-start.4 = (bf16[4,2,128,128]{3,2,1,0:T(8,128)(2,1)S(1)}, bf16[4,2,128,128]{3,2,1,0:T(8,128)(2,1)S(1)}, u32[]{:S(2)}, u32[]{:S(2)}) collective-permute-start(bf16[4,2,128,128]{3,2,1,0:T(8,128)(2,1)S(1)} %collective-permute-done.2.refs_0_), channel_id=1, source_target_pairs={{0,62},{1,63},{2,0},{3,1},{4,2},{5,3},{6,4},{7,5},{8,6},{9,7},{10,... | collective-permute-start | bytes 786440 | tf_op jit(solution)/shard_map/ppermute | solution.py:231
  79.6 3.8 %attend.5.refs_0_ = bf16[4,2,144,128]{3,2,1,0:T(8,128)(2,1)S(1)} custom-call(s32[16,1]{1,0:T(8,128)S(1)} %copy.44.pos_new, bf16[2,2048,256]{2,1,0:T(8,128)(2,1)S(1)} %copy-done.7, bf16[2,128,2048]{2,1,0:T(8,128)(2,1)S(1)} %copy-done.8, bf16[2,16,128]{2,1,0:T(8,128)(2,1)S(1)} %get-tuple-element.98.new_k, bf16[2,16,128]{2,1,0:T(8,128)(2,1)S(1)} %get-tuple-element.97.new_v, ...), custom_call_target="tpu_custom_call" | custom-call | flops 1610612736 | bytes 3670016 | tf_op jit(solution)/shard_map/attend/pallas_call | solution.py:134
  84.1 1.0 collective-permute-done.4.refs_0_
  85.1 3.1 %collective-permute-done.5.refs_1_ = bf16[4,2,128,128]{3,2,1,0:T(8,128)(2,1)S(1)} collective-permute-done((bf16[4,2,128,128]{3,2,1,0:T(8,128)(2,1)S(1)}, bf16[4,2,128,128]{3,2,1,0:T(8,128)(2,1)S(1)}, u32[]{:S(2)}, u32[]{:S(2)}) %collective-permute-start.5) | collective-permute-done | bytes 262176 | tf_op jit(solution)/shard_map/ppermute | solution.py:231
  88.5 1.2 collective-permute-start.7
  89.7 7.5 %attend.6 = (bf16[4,2,144,128]{3,2,1,0:T(8,128)(2,1)S(1)}, bf16[4,2,144,128]{3,2,1,0:T(8,128)(2,1)S(1)}) custom-call(s32[16,1]{1,0:T(8,128)S(1)} %copy.44.pos_new, bf16[2,2048,256]{2,1,0:T(8,128)(2,1)S(1)} %copy-done.7, bf16[2,128,2048]{2,1,0:T(8,128)(2,1)S(1)} %copy-done.8, bf16[2,16,128]{2,1,0:T(8,128)(2,1)S(1)} %get-tuple-element.98.new_k, ...), custom_call_target="tpu_custom_call" | custom-call | flops 3221225472 | bytes 4194304 | tf_op jit(solution)/shard_map/attend/pallas_call | solution.py:134
  97.3 0.7 copy-done.3
  98.0 0.7 copy-done.4
  98.7 1.9 collective-permute-start.8
  100.7 7.5 %attend.7 = (bf16[4,2,144,128]{3,2,1,0:T(8,128)(2,1)S(1)}, bf16[4,2,144,128]{3,2,1,0:T(8,128)(2,1)S(1)}) custom-call(s32[16,1]{1,0:T(8,128)S(1)} %copy.44.pos_new, bf16[2,2048,256]{2,1,0:T(8,128)(2,1)S(1)} %copy-done.7, bf16[2,128,2048]{2,1,0:T(8,128)(2,1)S(1)} %copy-done.8, bf16[2,16,128]{2,1,0:T(8,128)(2,1)S(1)} %get-tuple-element.98.new_k, ...), custom_call_target="tpu_custom_call" | custom-call | flops 3221225472 | bytes 4194304 | tf_op jit(solution)/shard_map/attend/pallas_call | solution.py:134
  109.0 3.8 %attend.9 = (bf16[2,2,144,128]{3,2,1,0:T(8,128)(2,1)S(1)}, bf16[2,2,144,128]{3,2,1,0:T(8,128)(2,1)S(1)}) custom-call(s32[16,1]{1,0:T(8,128)S(1)} %copy.44.pos_new, bf16[2,2048,256]{2,1,0:T(8,128)(2,1)S(1)} %copy-done.7, bf16[2,128,2048]{2,1,0:T(8,128)(2,1)S(1)} %copy-done.8, bf16[2,16,128]{2,1,0:T(8,128)(2,1)S(1)} %get-tuple-element.98.new_k, ...), custom_call_target="tpu_custom_call" | custom-call | flops 1610612736 | bytes 3670016 | tf_op jit(solution)/shard_map/attend/pallas_call | solution.py:134
  113.0 2.7 collective-permute-start.11
  115.7 7.5 %attend.8 = (bf16[4,2,144,128]{3,2,1,0:T(8,128)(2,1)S(1)}, bf16[4,2,144,128]{3,2,1,0:T(8,128)(2,1)S(1)}) custom-call(s32[16,1]{1,0:T(8,128)S(1)} %copy.44.pos_new, bf16[2,2048,256]{2,1,0:T(8,128)(2,1)S(1)} %copy-done.7, bf16[2,128,2048]{2,1,0:T(8,128)(2,1)S(1)} %copy-done.8, bf16[2,16,128]{2,1,0:T(8,128)(2,1)S(1)} %get-tuple-element.98.new_k, ...), custom_call_target="tpu_custom_call" | custom-call | flops 3221225472 | bytes 4194304 | tf_op jit(solution)/shard_map/attend/pallas_call | solution.py:134
  123.3 0.7 copy-done
  124.0 0.7 copy-done.1
  125.4 2.3 merge.4
  127.7 2.7 collective-permute-start.13
  130.4 4.3 %collective-permute-done.12.refs_1_ = bf16[4,2,144,128]{3,2,1,0:T(8,128)(2,1)S(1)} collective-permute-done((bf16[4,2,144,128]{3,2,1,0:T(8,128)(2,1)}, bf16[4,2,144,128]{3,2,1,0:T(8,128)(2,1)S(1)}, u32[]{:S(2)}, u32[]{:S(2)}) %collective-permute-start.12) | collective-permute-done | bytes 294944 | tf_op jit(solution)/shard_map/ppermute | solution.py:231
  134.7 0.7 copy-done.13
  136.2 2.6 merge.5
  138.8 2.7 collective-permute-start.15
  141.5 4.3 %collective-permute-done.14.refs_1_ = bf16[4,2,144,128]{3,2,1,0:T(8,128)(2,1)S(1)} collective-permute-done((bf16[4,2,144,128]{3,2,1,0:T(8,128)(2,1)}, bf16[4,2,144,128]{3,2,1,0:T(8,128)(2,1)S(1)}, u32[]{:S(2)}, u32[]{:S(2)}) %collective-permute-start.14) | collective-permute-done | bytes 294944 | tf_op jit(solution)/shard_map/ppermute | solution.py:231
  146.5 0.7 copy-done.16
  147.2 2.6 merge.6
  149.8 9.3 %collective-permute-start.16 = (bf16[4,2,144,128]{3,2,1,0:T(8,128)(2,1)}, bf16[4,2,144,128]{3,2,1,0:T(8,128)(2,1)S(1)}, u32[]{:S(2)}, u32[]{:S(2)}) collective-permute-start(bf16[4,2,144,128]{3,2,1,0:T(8,128)(2,1)} %get-tuple-element.59), channel_id=1, source_target_pairs={{0,2},{1,3},{2,4},{3,5},{4,6},{5,7},{6,8},{7,9},{8,10},{9,11},{10,... | collective-permute-start | bytes 884744 | tf_op jit(solution)/shard_map/ppermute | solution.py:231
  159.1 2.7 collective-permute-start.17
  161.7 4.3 %collective-permute-done.16.refs_1_ = bf16[4,2,144,128]{3,2,1,0:T(8,128)(2,1)S(1)} collective-permute-done((bf16[4,2,144,128]{3,2,1,0:T(8,128)(2,1)}, bf16[4,2,144,128]{3,2,1,0:T(8,128)(2,1)S(1)}, u32[]{:S(2)}, u32[]{:S(2)}) %collective-permute-start.16) | collective-permute-done | bytes 294944 | tf_op jit(solution)/shard_map/ppermute | solution.py:231
  166.1 0.7 copy-done.11
  167.5 2.2 merge.7
  169.7 1.6 constant_dynamic-slice_fusion.3
  171.4 2.2 collective-permute-start.19
  173.5 8.0 %collective-permute-start.20 = (bf16[1,2,144,128]{3,2,1,0:T(8,128)(2,1)S(1)}, bf16[1,2,144,128]{3,2,1,0:T(8,128)(2,1)S(1)}, u32[]{:S(2)}, u32[]{:S(2)}) collective-permute-start(bf16[1,2,144,128]{3,2,1,0:T(8,128)(2,1)S(1)} %get-tuple-element.71), channel_id=1, source_target_pairs={{0,48},{1,49},{2,50},{3,51},{4,52},{5,53},{6,54},{7,55},{8,56},{9,... | collective-permute-start | bytes 221192 | tf_op jit(solution)/shard_map/ppermute | solution.py:231
  181.5 9.9 %collective-permute-start.21 = (bf16[1,2,144,128]{3,2,1,0:T(8,128)(2,1)S(1)}, bf16[1,2,144,128]{3,2,1,0:T(8,128)(2,1)S(1)}, u32[]{:S(2)}, u32[]{:S(2)}) collective-permute-start(bf16[1,2,144,128]{3,2,1,0:T(8,128)(2,1)S(1)} %get-tuple-element.70), channel_id=1, source_target_pairs={{0,32},{1,33},{2,34},{3,35},{4,36},{5,37},{6,38},{7,39},{8,40},{9,... | collective-permute-start | bytes 221192 | tf_op jit(solution)/shard_map/ppermute | solution.py:231
  191.5 13.6 %collective-permute-done.21.refs_3_ = bf16[1,2,144,128]{3,2,1,0:T(8,128)(2,1)S(1)} collective-permute-done((bf16[1,2,144,128]{3,2,1,0:T(8,128)(2,1)S(1)}, bf16[1,2,144,128]{3,2,1,0:T(8,128)(2,1)S(1)}, u32[]{:S(2)}, u32[]{:S(2)}) %collective-permute-start.21) | collective-permute-done | bytes 73760 | tf_op jit(solution)/shard_map/ppermute | solution.py:231
  205.7 1.8 finish.1
  207.5 0.8 copy.67
  208.4 29.6 %all_gather.7 = bf16[4,8,4096]{2,1,0:T(8,128)(2,1)S(1)} all-gather(bf16[1,8,4096]{2,1,0:T(8,128)(2,1)S(1)} %all_gather_reshape.7), channel_id=1, replica_groups={{0,16,32,48},{1,17,33,49},{2,18,34,50},{3,19,35,51},{4,20,36,52},{5,21,..., dimensions={0}, use_global_device_ids=true | all-gather | bytes 327680 | tf_op jit(solution)/shard_map/all_gather | solution.py:251
  238.0 7.1 %collective-permute-start.23 = (bf16[4,8,4096]{2,1,0:T(8,128)(2,1)S(1)}, bf16[4,8,4096]{2,1,0:T(8,128)(2,1)S(1)}, u32[]{:S(2)}, u32[]{:S(2)}) collective-permute-start(bf16[4,8,4096]{2,1,0:T(8,128)(2,1)S(1)} %all_gather.7), channel_id=1, source_target_pairs={{0,62},{1,63},{2,0},{3,1},{4,2},{5,3},{6,4},{7,5},{8,6},{9,7},{10,... | collective-permute-start | bytes 786440 | tf_op jit(solution)/shard_map/ppermute | solution.py:231
  245.1 3.4 %collective-permute-done.23 = bf16[4,8,4096]{2,1,0:T(8,128)(2,1)S(1)} collective-permute-done((bf16[4,8,4096]{2,1,0:T(8,128)(2,1)S(1)}, bf16[4,8,4096]{2,1,0:T(8,128)(2,1)S(1)}, u32[]{:S(2)}, u32[]{:S(2)}) %collective-permute-start.23) | collective-permute-done | bytes 262176 | tf_op jit(solution)/shard_map/ppermute | solution.py:231
  248.5 3.0 %collective-permute-done.24 = bf16[4,8,4096]{2,1,0:T(8,128)(2,1)S(1)} collective-permute-done((bf16[4,8,4096]{2,1,0:T(8,128)(2,1)S(1)}, bf16[4,8,4096]{2,1,0:T(8,128)(2,1)S(1)}, u32[]{:S(2)}, u32[]{:S(2)}) %collective-permute-start.24) | collective-permute-done | bytes 262176 | tf_op jit(solution)/shard_map/ppermute | solution.py:231
  251.5 1.2 collective-permute-start.25
  253.0 10.0 %collective-permute-start.22 = (bf16[4,4096]{1,0:T(4,128)(2,1)S(1)}, bf16[4,4096]{1,0:T(4,128)(2,1)S(1)}, u32[]{:S(2)}, u32[]{:S(2)}) collective-permute-start(bf16[4,4096]{1,0:T(4,128)(2,1)S(1)} %get-tuple-element.77), channel_id=1, source_target_pairs={{0,1},{1,0},{2,3},{3,2},{4,5},{5,4},{6,7},{7,6},{8,9},{9,8},{10,11... | collective-permute-start | bytes 98312 | tf_op jit(solution)/shard_map/ppermute | solution.py:234
  263.1 3.0 %collective-permute-start.27 = (bf16[4,8,4096]{2,1,0:T(8,128)(2,1)}, bf16[4,8,4096]{2,1,0:T(8,128)(2,1)S(1)}, u32[]{:S(2)}, u32[]{:S(2)}) collective-permute-start(bf16[4,8,4096]{2,1,0:T(8,128)(2,1)} %collective-permute-done.25), channel_id=1, source_target_pairs={{0,62},{1,63},{2,0},{3,1},{4,2},{5,3},{6,4},{7,5},{8,6},{9,7},{10,... | collective-permute-start | bytes 786440 | tf_op jit(solution)/shard_map/ppermute | solution.py:231
  266.7 3.0 %collective-permute-done.27 = bf16[4,8,4096]{2,1,0:T(8,128)(2,1)S(1)} collective-permute-done((bf16[4,8,4096]{2,1,0:T(8,128)(2,1)}, bf16[4,8,4096]{2,1,0:T(8,128)(2,1)S(1)}, u32[]{:S(2)}, u32[]{:S(2)}) %collective-permute-start.27) | collective-permute-done | bytes 262176 | tf_op jit(solution)/shard_map/ppermute | solution.py:231
  269.7 3.0 %collective-permute-done.28 = bf16[4,8,4096]{2,1,0:T(8,128)(2,1)S(1)} collective-permute-done((bf16[4,8,4096]{2,1,0:T(8,128)(2,1)}, bf16[4,8,4096]{2,1,0:T(8,128)(2,1)S(1)}, u32[]{:S(2)}, u32[]{:S(2)}) %collective-permute-start.28) | collective-permute-done | bytes 262176 | tf_op jit(solution)/shard_map/ppermute | solution.py:231
  272.7 1.7 collective-permute-start.29
  274.4 1.0 constant_dynamic-update-slice_fusion.5
  275.5 1.0 constant_dynamic-update-slice_fusion.1
  277.2 1.0 collective-permute-done.29
  278.2 3.0 %collective-permute-done.30 = bf16[2,8,4096]{2,1,0:T(8,128)(2,1)S(1)} collective-permute-done((bf16[2,8,4096]{2,1,0:T(8,128)(2,1)S(1)}, bf16[2,8,4096]{2,1,0:T(8,128)(2,1)S(1)}, u32[]{:S(2)}, u32[]{:S(2)}) %collective-permute-start.30) | collective-permute-done | bytes 131104 | tf_op jit(solution)/shard_map/ppermute | solution.py:231
  281.7 8.9 %collective-permute-start.31 = (f32[256,256]{1,0:T(8,128)S(1)}, f32[256,256]{1,0:T(8,128)S(1)}, u32[]{:S(2)}, u32[]{:S(2)}) collective-permute-start(f32[256,256]{1,0:T(8,128)S(1)} %pad_maximum_fusion), channel_id=1, source_target_pairs={{0,1},{1,0},{2,3},{3,2},{4,5},{5,4},{6,7},{7,6},{8,9},{9,8},{10,11... | collective-permute-start | bytes 786440 | tf_op jit(solution)/shard_map/ppermute | solution.py:234
  (107 shorter events, 10.4 us)
Async XLA Ops:
  0.6 61.6 %collective-permute-start = (bf16[1024,1024]{1,0:T(8,128)(2,1)}, bf16[1024,1024]{1,0:T(8,128)(2,1)S(1)}, u32[]{:S(2)}, u32[]{:S(2)}) collective-permute-start(bf16[1024,1024]{1,0:T(8,128)(2,1)} %mine_v.1), channel_id=1, source_target_pairs={{0,1},{1,0},{2,3},{3,2},{4,5},{5,4},{6,7},{7,6},{8,9},{9,8},{10,11... | collective-permute-start | bytes 6291464 | tf_op jit(solution)/shard_map/ppermute | solution.py:234
  22.7 5.6 %collective-permute-start.1 = (bf16[4,4608]{1,0:T(4,128)(2,1)S(1)}, bf16[4,4608]{1,0:T(4,128)(2,1)S(1)}, u32[]{:S(2)}, u32[]{:S(2)}) collective-permute-start(bf16[4,4608]{1,0:T(4,128)(2,1)S(1)} %pad_maximum_fusion.1), channel_id=1, source_target_pairs={{0,1},{1,0},{2,3},{3,2},{4,5},{5,4},{6,7},{7,6},{8,9},{9,8},{10,11... | collective-permute-start | bytes 110600 | tf_op jit(solution)/shard_map/ppermute | solution.py:234
  56.5 20.1 %collective-permute-start.2 = (bf16[4,2,128,128]{3,2,1,0:T(8,128)(2,1)S(1)}, bf16[4,2,128,128]{3,2,1,0:T(8,128)(2,1)S(1)}, u32[]{:S(2)}, u32[]{:S(2)}) collective-permute-start(bf16[4,2,128,128]{3,2,1,0:T(8,128)(2,1)S(1)} %all_gather.6.refs_0_), channel_id=1, source_target_pairs={{0,62},{1,63},{2,0},{3,1},{4,2},{5,3},{6,4},{7,5},{8,6},{9,7},{10,... | collective-permute-start | bytes 786440 | tf_op jit(solution)/shard_map/ppermute | solution.py:231
  62.2 14.4 %collective-permute-start.3 = (bf16[4,2,128,128]{3,2,1,0:T(8,128)(2,1)S(1)}, bf16[4,2,128,128]{3,2,1,0:T(8,128)(2,1)S(1)}, u32[]{:S(2)}, u32[]{:S(2)}) collective-permute-start(bf16[4,2,128,128]{3,2,1,0:T(8,128)(2,1)S(1)} %all_gather.6.refs_0_), channel_id=1, source_target_pairs={{0,2},{1,3},{2,4},{3,5},{4,6},{5,7},{6,8},{7,9},{8,10},{9,11},{10,... | collective-permute-start | bytes 786440 | tf_op jit(solution)/shard_map/ppermute | solution.py:231
  62.3 1.3 copy-start.10
  67.4 12.1 %copy-start.7 = (bf16[2,2048,256]{2,1,0:T(8,128)(2,1)S(1)}, bf16[2,2048,256]{2,1,0:T(8,128)(2,1)}, u32[]{:S(2)}) copy-start(bf16[2,2048,256]{2,1,0:T(8,128)(2,1)} %get-tuple-element.36.keys_ref) | copy-start | bytes 6291460
  67.4 12.1 %copy-start.8 = (bf16[2,128,2048]{2,1,0:T(8,128)(2,1)S(1)}, bf16[2,128,2048]{2,1,0:T(8,128)(2,1)}, u32[]{:S(2)}) copy-start(bf16[2,128,2048]{2,1,0:T(8,128)(2,1)} %get-tuple-element.37.values_ref) | copy-start | bytes 3145732
  70.7 99.0 %collective-permute-start.18 = (bf16[4096,256]{1,0:T(8,128)(2,1)}, bf16[4096,256]{1,0:T(8,128)(2,1)S(1)}, u32[]{:S(2)}, u32[]{:S(2)}) collective-permute-start(bf16[4096,256]{1,0:T(8,128)(2,1)} %constant_dynamic-slice_fusion.14), channel_id=1, source_target_pairs={{0,1},{1,0},{2,3},{3,2},{4,5},{5,4},{6,7},{7,6},{8,9},{9,8},{10,11... | collective-permute-start | bytes 6291464 | tf_op jit(solution)/shard_map/ppermute | solution.py:234
  76.6 8.5 %collective-permute-start.4 = (bf16[4,2,128,128]{3,2,1,0:T(8,128)(2,1)S(1)}, bf16[4,2,128,128]{3,2,1,0:T(8,128)(2,1)S(1)}, u32[]{:S(2)}, u32[]{:S(2)}) collective-permute-start(bf16[4,2,128,128]{3,2,1,0:T(8,128)(2,1)S(1)} %collective-permute-done.2.refs_0_), channel_id=1, source_target_pairs={{0,62},{1,63},{2,0},{3,1},{4,2},{5,3},{6,4},{7,5},{8,6},{9,7},{10,... | collective-permute-start | bytes 786440 | tf_op jit(solution)/shard_map/ppermute | solution.py:231
  79.6 8.7 %collective-permute-start.5 = (bf16[4,2,128,128]{3,2,1,0:T(8,128)(2,1)S(1)}, bf16[4,2,128,128]{3,2,1,0:T(8,128)(2,1)S(1)}, u32[]{:S(2)}, u32[]{:S(2)}) collective-permute-start(bf16[4,2,128,128]{3,2,1,0:T(8,128)(2,1)S(1)} %collective-permute-done.3.refs_1_), channel_id=1, source_target_pairs={{0,2},{1,3},{2,4},{3,5},{4,6},{5,7},{6,8},{7,9},{8,10},{9,11},{10,... | collective-permute-start | bytes 786440 | tf_op jit(solution)/shard_map/ppermute | solution.py:231
  83.4 0.7 copy-start.2
  88.3 10.5 %collective-permute-start.6 = (bf16[4,2,128,128]{3,2,1,0:T(8,128)(2,1)S(1)}, bf16[4,2,128,128]{3,2,1,0:T(8,128)(2,1)S(1)}, u32[]{:S(2)}, u32[]{:S(2)}) collective-permute-start(bf16[4,2,128,128]{3,2,1,0:T(8,128)(2,1)S(1)} %collective-permute-done.4.refs_0_), channel_id=1, source_target_pairs={{0,62},{1,63},{2,0},{3,1},{4,2},{5,3},{6,4},{7,5},{8,6},{9,7},{10,... | collective-permute-start | bytes 786440 | tf_op jit(solution)/shard_map/ppermute | solution.py:231
  88.5 10.2 %collective-permute-start.7 = (bf16[4,2,128,128]{3,2,1,0:T(8,128)(2,1)S(1)}, bf16[4,2,128,128]{3,2,1,0:T(8,128)(2,1)S(1)}, u32[]{:S(2)}, u32[]{:S(2)}) collective-permute-start(bf16[4,2,128,128]{3,2,1,0:T(8,128)(2,1)S(1)} %collective-permute-done.5.refs_1_), channel_id=1, source_target_pairs={{0,2},{1,3},{2,4},{3,5},{4,6},{5,7},{6,8},{7,9},{8,10},{9,11},{10,... | collective-permute-start | bytes 786440 | tf_op jit(solution)/shard_map/ppermute | solution.py:231
  97.2 0.7 copy-start.3
  98.0 0.7 copy-start.4
  98.7 10.3 %collective-permute-start.8 = (bf16[2,2,128,128]{3,2,1,0:T(8,128)(2,1)S(1)}, bf16[2,2,128,128]{3,2,1,0:T(8,128)(2,1)S(1)}, u32[]{:S(2)}, u32[]{:S(2)}) collective-permute-start(bf16[2,2,128,128]{3,2,1,0:T(8,128)(2,1)S(1)} %slice.40), channel_id=1, source_target_pairs={{0,62},{1,63},{2,0},{3,1},{4,2},{5,3},{6,4},{7,5},{8,6},{9,7},{10,... | collective-permute-start | bytes 393224 | tf_op jit(solution)/shard_map/ppermute | solution.py:231
  100.6 8.4 %collective-permute-start.9 = (bf16[2,2,128,128]{3,2,1,0:T(8,128)(2,1)S(1)}, bf16[2,2,128,128]{3,2,1,0:T(8,128)(2,1)S(1)}, u32[]{:S(2)}, u32[]{:S(2)}) collective-permute-start(bf16[2,2,128,128]{3,2,1,0:T(8,128)(2,1)S(1)} %slice.41), channel_id=1, source_target_pairs={{0,2},{1,3},{2,4},{3,5},{4,6},{5,7},{6,8},{7,9},{8,10},{9,11},{10,... | collective-permute-start | bytes 393224 | tf_op jit(solution)/shard_map/ppermute | solution.py:231
  108.3 0.7 copy-start.5
  109.0 3.9 %copy-start.6 = (bf16[4,2,144,128]{3,2,1,0:T(8,128)(2,1)}, bf16[4,2,144,128]{3,2,1,0:T(8,128)(2,1)S(1)}, u32[]{:S(2)}) copy-start(bf16[4,2,144,128]{3,2,1,0:T(8,128)(2,1)S(1)} %get-tuple-element.49.refs_2_) | copy-start | bytes 884740
  112.9 11.9 %collective-permute-start.10 = (bf16[2,2,144,128]{3,2,1,0:T(8,128)(2,1)S(1)}, bf16[2,2,144,128]{3,2,1,0:T(8,128)(2,1)S(1)}, u32[]{:S(2)}, u32[]{:S(2)}) collective-permute-start(bf16[2,2,144,128]{3,2,1,0:T(8,128)(2,1)S(1)} %get-tuple-element.52), channel_id=1, source_target_pairs={{0,2},{1,3},{2,4},{3,5},{4,6},{5,7},{6,8},{7,9},{8,10},{9,11},{10,... | collective-permute-start | bytes 442376 | tf_op jit(solution)/shard_map/ppermute | solution.py:231
  113.0 11.7 %collective-permute-start.11 = (bf16[2,2,144,128]{3,2,1,0:T(8,128)(2,1)S(1)}, bf16[2,2,144,128]{3,2,1,0:T(8,128)(2,1)S(1)}, u32[]{:S(2)}, u32[]{:S(2)}) collective-permute-start(bf16[2,2,144,128]{3,2,1,0:T(8,128)(2,1)S(1)} %get-tuple-element.54), channel_id=1, source_target_pairs={{0,62},{1,63},{2,0},{3,1},{4,2},{5,3},{6,4},{7,5},{8,6},{9,7},{10,... | collective-permute-start | bytes 442376 | tf_op jit(solution)/shard_map/ppermute | solution.py:231
  123.3 0.7 copy-start
  124.0 0.7 copy-start.1
  124.7 0.7 copy-start.17
  124.7 0.7 copy-start.18
  127.7 7.0 %collective-permute-start.12 = (bf16[4,2,144,128]{3,2,1,0:T(8,128)(2,1)}, bf16[4,2,144,128]{3,2,1,0:T(8,128)(2,1)S(1)}, u32[]{:S(2)}, u32[]{:S(2)}) collective-permute-start(bf16[4,2,144,128]{3,2,1,0:T(8,128)(2,1)} %get-tuple-element.55), channel_id=1, source_target_pairs={{0,2},{1,3},{2,4},{3,5},{4,6},{5,7},{6,8},{7,9},{8,10},{9,11},{10,... | collective-permute-start | bytes 884744 | tf_op jit(solution)/shard_map/ppermute | solution.py:231
  127.7 7.0 %collective-permute-start.13 = (bf16[4,2,144,128]{3,2,1,0:T(8,128)(2,1)}, bf16[4,2,144,128]{3,2,1,0:T(8,128)(2,1)S(1)}, u32[]{:S(2)}, u32[]{:S(2)}) collective-permute-start(bf16[4,2,144,128]{3,2,1,0:T(8,128)(2,1)} %get-tuple-element.56), channel_id=1, source_target_pairs={{0,62},{1,63},{2,0},{3,1},{4,2},{5,3},{6,4},{7,5},{8,6},{9,7},{10,... | collective-permute-start | bytes 884744 | tf_op jit(solution)/shard_map/ppermute | solution.py:231
  134.7 0.7 copy-start.13
  135.4 0.7 copy-start.15
  138.8 7.0 %collective-permute-start.14 = (bf16[4,2,144,128]{3,2,1,0:T(8,128)(2,1)}, bf16[4,2,144,128]{3,2,1,0:T(8,128)(2,1)S(1)}, u32[]{:S(2)}, u32[]{:S(2)}) collective-permute-start(bf16[4,2,144,128]{3,2,1,0:T(8,128)(2,1)} %get-tuple-element.57), channel_id=1, source_target_pairs={{0,2},{1,3},{2,4},{3,5},{4,6},{5,7},{6,8},{7,9},{8,10},{9,11},{10,... | collective-permute-start | bytes 884744 | tf_op jit(solution)/shard_map/ppermute | solution.py:231
  138.8 7.0 %collective-permute-start.15 = (bf16[4,2,144,128]{3,2,1,0:T(8,128)(2,1)}, bf16[4,2,144,128]{3,2,1,0:T(8,128)(2,1)S(1)}, u32[]{:S(2)}, u32[]{:S(2)}) collective-permute-start(bf16[4,2,144,128]{3,2,1,0:T(8,128)(2,1)} %get-tuple-element.58), channel_id=1, source_target_pairs={{0,62},{1,63},{2,0},{3,1},{4,2},{5,3},{6,4},{7,5},{8,6},{9,7},{10,... | collective-permute-start | bytes 884744 | tf_op jit(solution)/shard_map/ppermute | solution.py:231
  145.8 0.7 copy-start.14
  146.5 0.7 copy-start.16
  149.8 16.3 %collective-permute-start.16 = (bf16[4,2,144,128]{3,2,1,0:T(8,128)(2,1)}, bf16[4,2,144,128]{3,2,1,0:T(8,128)(2,1)S(1)}, u32[]{:S(2)}, u32[]{:S(2)}) collective-permute-start(bf16[4,2,144,128]{3,2,1,0:T(8,128)(2,1)} %get-tuple-element.59), channel_id=1, source_target_pairs={{0,2},{1,3},{2,4},{3,5},{4,6},{5,7},{6,8},{7,9},{8,10},{9,11},{10,... | collective-permute-start | bytes 884744 | tf_op jit(solution)/shard_map/ppermute | solution.py:231
  159.1 7.0 %collective-permute-start.17 = (bf16[4,2,144,128]{3,2,1,0:T(8,128)(2,1)}, bf16[4,2,144,128]{3,2,1,0:T(8,128)(2,1)S(1)}, u32[]{:S(2)}, u32[]{:S(2)}) collective-permute-start(bf16[4,2,144,128]{3,2,1,0:T(8,128)(2,1)} %get-tuple-element.60), channel_id=1, source_target_pairs={{0,62},{1,63},{2,0},{3,1},{4,2},{5,3},{6,4},{7,5},{8,6},{9,7},{10,... | collective-permute-start | bytes 884744 | tf_op jit(solution)/shard_map/ppermute | solution.py:231
  166.0 0.7 copy-start.11
  166.8 0.7 copy-start.12
  171.4 20.1 %collective-permute-start.19 = (bf16[1,2,144,128]{3,2,1,0:T(8,128)(2,1)S(1)}, bf16[1,2,144,128]{3,2,1,0:T(8,128)(2,1)S(1)}, u32[]{:S(2)}, u32[]{:S(2)}) collective-permute-start(bf16[1,2,144,128]{3,2,1,0:T(8,128)(2,1)S(1)} %get-tuple-element.72), channel_id=1, source_target_pairs={{0,16},{1,17},{2,18},{3,19},{4,20},{5,21},{6,22},{7,23},{8,24},{9,... | collective-permute-start | bytes 221192 | tf_op jit(solution)/shard_map/ppermute | solution.py:231
  173.5 17.9 %collective-permute-start.20 = (bf16[1,2,144,128]{3,2,1,0:T(8,128)(2,1)S(1)}, bf16[1,2,144,128]{3,2,1,0:T(8,128)(2,1)S(1)}, u32[]{:S(2)}, u32[]{:S(2)}) collective-permute-start(bf16[1,2,144,128]{3,2,1,0:T(8,128)(2,1)S(1)} %get-tuple-element.71), channel_id=1, source_target_pairs={{0,48},{1,49},{2,50},{3,51},{4,52},{5,53},{6,54},{7,55},{8,56},{9,... | collective-permute-start | bytes 221192 | tf_op jit(solution)/shard_map/ppermute | solution.py:231
  181.5 23.6 %collective-permute-start.21 = (bf16[1,2,144,128]{3,2,1,0:T(8,128)(2,1)S(1)}, bf16[1,2,144,128]{3,2,1,0:T(8,128)(2,1)S(1)}, u32[]{:S(2)}, u32[]{:S(2)}) collective-permute-start(bf16[1,2,144,128]{3,2,1,0:T(8,128)(2,1)S(1)} %get-tuple-element.70), channel_id=1, source_target_pairs={{0,32},{1,33},{2,34},{3,35},{4,36},{5,37},{6,38},{7,39},{8,40},{9,... | collective-permute-start | bytes 221192 | tf_op jit(solution)/shard_map/ppermute | solution.py:231
  191.4 13.7 %copy-start.19 = (bf16[1,2,144,128]{3,2,1,0:T(8,128)(2,1)}, bf16[1,2,144,128]{3,2,1,0:T(8,128)(2,1)S(1)}, u32[]{:S(2)}) copy-start(bf16[1,2,144,128]{3,2,1,0:T(8,128)(2,1)S(1)} %collective-permute-done.19.refs_1_) | copy-start | bytes 221188
  191.4 13.7 %copy-start.20 = (bf16[1,2,144,128]{3,2,1,0:T(8,128)(2,1)}, bf16[1,2,144,128]{3,2,1,0:T(8,128)(2,1)S(1)}, u32[]{:S(2)}) copy-start(bf16[1,2,144,128]{3,2,1,0:T(8,128)(2,1)S(1)} %collective-permute-done.20.refs_2_) | copy-start | bytes 221188
  205.1 0.6 copy-start.21
  238.0 10.5 %collective-permute-start.23 = (bf16[4,8,4096]{2,1,0:T(8,128)(2,1)S(1)}, bf16[4,8,4096]{2,1,0:T(8,128)(2,1)S(1)}, u32[]{:S(2)}, u32[]{:S(2)}) collective-permute-start(bf16[4,8,4096]{2,1,0:T(8,128)(2,1)S(1)} %all_gather.7), channel_id=1, source_target_pairs={{0,62},{1,63},{2,0},{3,1},{4,2},{5,3},{6,4},{7,5},{8,6},{9,7},{10,... | collective-permute-start | bytes 786440 | tf_op jit(solution)/shard_map/ppermute | solution.py:231
  245.1 6.4 %collective-permute-start.24 = (bf16[4,8,4096]{2,1,0:T(8,128)(2,1)S(1)}, bf16[4,8,4096]{2,1,0:T(8,128)(2,1)S(1)}, u32[]{:S(2)}, u32[]{:S(2)}) collective-permute-start(bf16[4,8,4096]{2,1,0:T(8,128)(2,1)S(1)} %all_gather.7), channel_id=1, source_target_pairs={{0,2},{1,3},{2,4},{3,5},{4,6},{5,7},{6,8},{7,9},{8,10},{9,11},{10,... | collective-permute-start | bytes 786440 | tf_op jit(solution)/shard_map/ppermute | solution.py:231
  251.5 11.5 %collective-permute-start.25 = (bf16[4,8,4096]{2,1,0:T(8,128)(2,1)S(1)}, bf16[4,8,4096]{2,1,0:T(8,128)(2,1)}, u32[]{:S(2)}, u32[]{:S(2)}) collective-permute-start(bf16[4,8,4096]{2,1,0:T(8,128)(2,1)S(1)} %collective-permute-done.23), channel_id=1, source_target_pairs={{0,62},{1,63},{2,0},{3,1},{4,2},{5,3},{6,4},{7,5},{8,6},{9,7},{10,... | collective-permute-start | bytes 786440 | tf_op jit(solution)/shard_map/ppermute | solution.py:231
  252.8 10.3 %collective-permute-start.26 = (bf16[4,8,4096]{2,1,0:T(8,128)(2,1)S(1)}, bf16[4,8,4096]{2,1,0:T(8,128)(2,1)}, u32[]{:S(2)}, u32[]{:S(2)}) collective-permute-start(bf16[4,8,4096]{2,1,0:T(8,128)(2,1)S(1)} %collective-permute-done.24), channel_id=1, source_target_pairs={{0,2},{1,3},{2,4},{3,5},{4,6},{5,7},{6,8},{7,9},{8,10},{9,11},{10,... | collective-permute-start | bytes 786440 | tf_op jit(solution)/shard_map/ppermute | solution.py:231
  253.0 13.0 %collective-permute-start.22 = (bf16[4,4096]{1,0:T(4,128)(2,1)S(1)}, bf16[4,4096]{1,0:T(4,128)(2,1)S(1)}, u32[]{:S(2)}, u32[]{:S(2)}) collective-permute-start(bf16[4,4096]{1,0:T(4,128)(2,1)S(1)} %get-tuple-element.77), channel_id=1, source_target_pairs={{0,1},{1,0},{2,3},{3,2},{4,5},{5,4},{6,7},{7,6},{8,9},{9,8},{10,11... | collective-permute-start | bytes 98312 | tf_op jit(solution)/shard_map/ppermute | solution.py:234
  263.1 6.6 %collective-permute-start.27 = (bf16[4,8,4096]{2,1,0:T(8,128)(2,1)}, bf16[4,8,4096]{2,1,0:T(8,128)(2,1)S(1)}, u32[]{:S(2)}, u32[]{:S(2)}) collective-permute-start(bf16[4,8,4096]{2,1,0:T(8,128)(2,1)} %collective-permute-done.25), channel_id=1, source_target_pairs={{0,62},{1,63},{2,0},{3,1},{4,2},{5,3},{6,4},{7,5},{8,6},{9,7},{10,... | collective-permute-start | bytes 786440 | tf_op jit(solution)/shard_map/ppermute | solution.py:231
  266.0 6.6 %collective-permute-start.28 = (bf16[4,8,4096]{2,1,0:T(8,128)(2,1)}, bf16[4,8,4096]{2,1,0:T(8,128)(2,1)S(1)}, u32[]{:S(2)}, u32[]{:S(2)}) collective-permute-start(bf16[4,8,4096]{2,1,0:T(8,128)(2,1)} %collective-permute-done.26), channel_id=1, source_target_pairs={{0,2},{1,3},{2,4},{3,5},{4,6},{5,7},{6,8},{7,9},{8,10},{9,11},{10,... | collective-permute-start | bytes 786440 | tf_op jit(solution)/shard_map/ppermute | solution.py:231
  272.7 5.4 %collective-permute-start.29 = (bf16[2,8,4096]{2,1,0:T(8,128)(2,1)S(1)}, bf16[2,8,4096]{2,1,0:T(8,128)(2,1)S(1)}, u32[]{:S(2)}, u32[]{:S(2)}) collective-permute-start(bf16[2,8,4096]{2,1,0:T(8,128)(2,1)S(1)} %slice.46), channel_id=1, source_target_pairs={{0,62},{1,63},{2,0},{3,1},{4,2},{5,3},{6,4},{7,5},{8,6},{9,7},{10,... | collective-permute-start | bytes 393224 | tf_op jit(solution)/shard_map/ppermute | solution.py:231
  274.4 6.7 %collective-permute-start.30 = (bf16[2,8,4096]{2,1,0:T(8,128)(2,1)S(1)}, bf16[2,8,4096]{2,1,0:T(8,128)(2,1)S(1)}, u32[]{:S(2)}, u32[]{:S(2)}) collective-permute-start(bf16[2,8,4096]{2,1,0:T(8,128)(2,1)S(1)} %slice.47), channel_id=1, source_target_pairs={{0,2},{1,3},{2,4},{3,5},{4,6},{5,7},{6,8},{7,9},{8,10},{9,11},{10,... | collective-permute-start | bytes 393224 | tf_op jit(solution)/shard_map/ppermute | solution.py:231
  276.5 14.0 %copy-start.9 = (bf16[8192,256]{1,0:T(8,128)(2,1)S(1)}, bf16[8192,256]{1,0:T(8,128)(2,1)}, u32[]{:S(2)}) copy-start(bf16[8192,256]{1,0:T(8,128)(2,1)} %param.11) | copy-start | bytes 12582916
  281.7 10.0 %collective-permute-start.31 = (f32[256,256]{1,0:T(8,128)S(1)}, f32[256,256]{1,0:T(8,128)S(1)}, u32[]{:S(2)}, u32[]{:S(2)}) collective-permute-start(f32[256,256]{1,0:T(8,128)S(1)} %pad_maximum_fusion), channel_id=1, source_target_pairs={{0,1},{1,0},{2,3},{3,2},{4,5},{5,4},{6,7},{7,6},{8,9},{9,8},{10,11... | collective-permute-start | bytes 786440 | tf_op jit(solution)/shard_map/ppermute | solution.py:234

commit v2 on v0

--- a/solution.py
+++ b/solution.py
@@ -184,18 +184,19 @@
     )(*arrays)
 
 
-def finish_body(parts_ref, out_ref):
+def finish_body(*refs):
+    out_ref = refs[-1]
     for g in range(out_ref.shape[0]):
-        out, _ = merged([(parts_ref[k, g, :HD, :], parts_ref[k, g, HD:, :]) for k in range(parts_ref.shape[0])])
+        out, _ = merged([(r[0, g, :HD, :], r[0, g, HD:, :]) for r in refs[:-1]])
         out_ref[g] = out.T.astype(jnp.bfloat16)
 
 
-def finish(parts):
+def finish(*arrays):
     return pl.pallas_call(
         finish_body,
         out_shape=jax.ShapeDtypeStruct((KVH // 2, HD, HD), jnp.bfloat16),
         name="finish",
-    )(parts)
+    )(*arrays)
 
 
 def shards(queries, new_kv, prefix_cache, positions, lengths, out_weight):
@@ -275,7 +276,14 @@
     right, left = after(w_theirs, right, left)
     right, left = take(right, -1), take(left, 1)
     (summed,) = merge([(parts[0], 0, 0), (right, 0, 0), (left, 0, 0)])
-    own = finish(lax.all_to_all(summed, CTX, 0, 0, axis_index_groups=classes, tiled=True))
+    piece = lambda d: lax.dynamic_slice_in_dim(summed, (chip // HOP + d) % ring, 1, 0)
+    high = ring // 2
+    up, down = take(piece(high)[:, :1], -HOP), take(piece(high)[:, 1:], HOP)
+    for k in range(high - 1, 0, -1):
+        start = 1 if k == high - 1 else 0
+        up, down = merge([(piece(k), 0, 0), (up, 0, 0)], [(piece(ring - k), 0, 0), (down, 0, start)])
+        up, down = take(up, -HOP), take(down, HOP)
+    own = finish(piece(0), up, down)
     rows = own.reshape(KVH // 2, 2 * tokens, per_group, HD).transpose(1, 0, 2, 3).reshape(2 * tokens, half)
 
     keep = lax.dynamic_slice_in_dim(rows, core * tokens, tokens, 0)

time: 281 us -> 270 us (0.961)
  waiting for transfers between devices: 78.1 us -> 40.7 us
  starting transfers between devices: 55.4 us -> 78.3 us
  blocking collectives: 79 us -> 74 us
  Pallas kernels: 41.4 us -> 46.3 us
  local copies, waits for them, and re-layouts: 15.8 us -> 20.2 us
    all_to_all x1 -> x0, waiting for transfers between devices: 58.8 us -> none  [shards(): lax.all_to_all(summed, CTX, 0, 0, axis_index_groups=classes, tiled=True)]
    ppermute x12 -> x20, starting transfers between devices: 17.6 us -> 39.3 us  [take(): lax.ppermute(x, CTX, [(i, (i - 2 * d) % devices) for i in range(devices)])]
    ppermute x12 -> x20, waiting for transfers between devices: 19.2 us -> 40.5 us  [take(): lax.ppermute(x, CTX, [(i, (i - 2 * d) % devices) for i in range(devices)])]
    ppermute x5, starting transfers between devices: 27.7 us -> 39 us  [swap(): return lax.ppermute(x, CTX, [(i, i ^ 1) for i in range(devices)])]
    all_to_all x1 -> x0, starting transfers between devices: 10.2 us -> none  [shards(): lax.all_to_all(summed, CTX, 0, 0, axis_index_groups=classes, tiled=True)]
    all_gather x2, blocking collectives: 79 us -> 74 us  [gathered(): own = lax.all_gather(block, CTX, axis_index_groups=classes)]
    pallas_call x2 -> x5, Pallas kernels: 6.1 us -> 11.1 us  [merge(): pl.pallas_call(functools.partial(merge_body, starts), out_shape=[jax.Shap...]
    unnamed x31 -> x45, local copies, waits for them, and re-layouts: 9.25 us -> 10.9 us
  transfers between devices with their start and end apart: 18 -> 25, of which waited for: 6 -> 12; matrix products, arithmetic and copies ran while one was open for 4% -> 5% of each run, Pallas kernels for 13% -> 14%
where the time goes in v2:
time: 270 us; the launch traced here: 269 us
  starting transfers between devices  78.3 us (29%)
  blocking collectives  74 us (27%)
  Pallas kernels  46.3 us (17%)
  waiting for transfers between devices  40.7 us (15%)
  local copies, waits for them, and re-layouts  20.2 us (7%)
  matrix products  5.47 us (2%)
  other arithmetic  2.86 us (1%)
    all_gather x2, blocking collectives, gathered(): own = lax.all_gather(block, CTX, axis_index_groups=classes)  74 us
    ppermute x20, waiting for transfers between devices, take(): lax.ppermute(x, CTX, [(i, (i - 2 * d) % devices) for i in range(devices)])  40.5 us
    ppermute x20, starting transfers between devices, take(): lax.ppermute(x, CTX, [(i, (i - 2 * d) % devices) for i in range(devices)])  39.3 us
    ppermute x5, starting transfers between devices, swap(): return lax.ppermute(x, CTX, [(i, i ^ 1) for i in range(devices)])  39 us
    pallas_call x4, Pallas kernels, attend(): pl.pallas_call(attend_body, grid=(KVH // 2,), in_specs=[whole(pos_new), p...  29.5 us
    pallas_call x5, Pallas kernels, merge(): pl.pallas_call(functools.partial(merge_body, starts), out_shape=[jax.Shap...  11.1 us
    unnamed x45, local copies, waits for them, and re-layouts  10.9 us
  transfers between devices with their start and end apart: 25, of which 12 were waited for; matrix products, arithmetic and copies ran while one was open for 5% of the time, Pallas kernels for 14%

profile of v2, /device:TPU:37, one launch (start us, length us, event | category | flops | bytes accessed | tf_op | source)
XLA Modules:
  0.0 268.7 jit_solution(15532623153035580764)
XLA Ops:
  0.6 20.5 %collective-permute-start = (bf16[1024,1024]{1,0:T(8,128)(2,1)}, bf16[1024,1024]{1,0:T(8,128)(2,1)}, u32[]{:S(2)}, u32[]{:S(2)}) collective-permute-start(bf16[1024,1024]{1,0:T(8,128)(2,1)} %mine_v.1), channel_id=1, source_target_pairs={{0,1},{1,0},{2,3},{3,2},{4,5},{5,4},{6,7},{7,6},{8,9},{9,8},{10,11... | collective-permute-start | bytes 6291464 | tf_op jit(solution)/shard_map/ppermute | solution.py:216
  21.2 0.7 constant_dynamic-slice_fusion.19
  21.9 0.8 dynamic-slice_bitcast_fusion
  22.9 3.1 %constant_dynamic-slice_fusion.12 = bf16[4096,256]{1,0:T(8,128)(2,1)} fusion(bf16[8192,256]{1,0:T(8,128)(2,1)} %param.11, s32[]{:T(128)S(6)} %select_n.174), kind=kLoop, calls=%fused_computation.41 | loop fusion | bytes 4194308 | tf_op jit(solution)/shard_map/dynamic_slice | solution.py:260
  27.6 1.9 pad_add_fusion.1.lens_ref
  29.7 36.8 %all_gather.6.refs_0_ = bf16[8,2,128,128]{3,2,1,0:T(8,128)(2,1)S(1)} all-gather(bf16[1,2,128,128]{3,2,1,0:T(8,128)(2,1)S(1)} %bitcast.67), channel_id=1, replica_groups={{0,8,16,24,32,40,48,56},{1,9,17,25,33,41,49,57},{2,10,18,26,34,42,50,58..., dimensions={0}, use_global_device_ids=true | all-gather | bytes 589824 | tf_op jit(solution)/shard_map/all_gather | solution.py:233
  66.5 3.1 %collective-permute-start.2 = (bf16[8,2,128,128]{3,2,1,0:T(8,128)(2,1)S(1)}, bf16[8,2,128,128]{3,2,1,0:T(8,128)(2,1)S(1)}, u32[]{:S(2)}, u32[]{:S(2)}) collective-permute-start(bf16[8,2,128,128]{3,2,1,0:T(8,128)(2,1)S(1)} %all_gather.6.refs_0_), channel_id=1, source_target_pairs={{0,62},{1,63},{2,0},{3,1},{4,2},{5,3},{6,4},{7,5},{8,6},{9,7},{10,... | collective-permute-start | bytes 1572872 | tf_op jit(solution)/shard_map/ppermute | solution.py:213
  69.6 3.9 %prepare.1 = (bf16[2,2048,256]{2,1,0:T(8,128)(2,1)}, bf16[2,128,2048]{2,1,0:T(8,128)(2,1)}) custom-call(s32[3]{0:T(128)} %pad_add_fusion.1.lens_ref, bf16[1024,1024]{1,0:T(8,128)(2,1)} %mine_v.1, bf16[1024,1024]{1,0:T(8,128)(2,1)} %mine_v.1, bf16[1024,1024]{1,0:T(8,128)(2,1)} %collective-permute-done.theirs_k.theirs_v, ...), custom_call_target="tpu_custom_call" | custom-call | flops 268435456 | bytes 5242880 | tf_op jit(solution)/shard_map/prepare/pallas_call | solution.py:39
  73.6 1.6 copy-done.3
  75.2 1.2 copy-done.4
  76.4 7.4 %attend.4.refs_0_ = bf16[8,2,144,128]{3,2,1,0:T(8,128)(2,1)S(1)} custom-call(s32[16,1]{1,0:T(8,128)S(1)} %copy.41.pos_new, bf16[2,2048,256]{2,1,0:T(8,128)(2,1)S(1)} %copy-done.3, bf16[2,128,2048]{2,1,0:T(8,128)(2,1)S(1)} %copy-done.4, bf16[2,16,128]{2,1,0:T(8,128)(2,1)S(1)} %get-tuple-element.71.new_k, bf16[2,16,128]{2,1,0:T(8,128)(2,1)S(1)} %get-tuple-element.70.new_v, ...), custom_call_target="tpu_custom_call" | custom-call | flops 3221225472 | bytes 4194304 | tf_op jit(solution)/shard_map/attend/pallas_call | solution.py:122
  83.9 2.8 %collective-permute-start.4 = (bf16[4,2,128,128]{3,2,1,0:T(8,128)(2,1)S(1)}, bf16[4,2,128,128]{3,2,1,0:T(8,128)(2,1)S(1)}, u32[]{:S(2)}, u32[]{:S(2)}) collective-permute-start(bf16[4,2,128,128]{3,2,1,0:T(8,128)(2,1)S(1)} %slice.46), channel_id=1, source_target_pairs={{0,62},{1,63},{2,0},{3,1},{4,2},{5,3},{6,4},{7,5},{8,6},{9,7},{10,... | collective-permute-start | bytes 786440 | tf_op jit(solution)/shard_map/ppermute | solution.py:213
  87.0 7.5 %attend.5.refs_0_ = bf16[8,2,144,128]{3,2,1,0:T(8,128)(2,1)S(1)} custom-call(s32[16,1]{1,0:T(8,128)S(1)} %copy.41.pos_new, bf16[2,2048,256]{2,1,0:T(8,128)(2,1)S(1)} %copy-done.3, bf16[2,128,2048]{2,1,0:T(8,128)(2,1)S(1)} %copy-done.4, bf16[2,16,128]{2,1,0:T(8,128)(2,1)S(1)} %get-tuple-element.71.new_k, bf16[2,16,128]{2,1,0:T(8,128)(2,1)S(1)} %get-tuple-element.70.new_v, ...), custom_call_target="tpu_custom_call" | custom-call | flops 3221225472 | bytes 4194304 | tf_op jit(solution)/shard_map/attend/pallas_call | solution.py:122
  94.5 0.8 copy-done
  95.3 7.2 %attend.6 = (bf16[4,2,144,128]{3,2,1,0:T(8,128)(2,1)S(1)}, bf16[4,2,144,128]{3,2,1,0:T(8,128)(2,1)S(1)}) custom-call(s32[16,1]{1,0:T(8,128)S(1)} %copy.41.pos_new, bf16[2,2048,256]{2,1,0:T(8,128)(2,1)S(1)} %copy-done.3, bf16[2,128,2048]{2,1,0:T(8,128)(2,1)S(1)} %copy-done.4, bf16[2,16,128]{2,1,0:T(8,128)(2,1)S(1)} %get-tuple-element.71.new_k, ...), custom_call_target="tpu_custom_call" | custom-call | flops 3221225472 | bytes 4194304 | tf_op jit(solution)/shard_map/attend/pallas_call | solution.py:122
  102.6 2.7 %collective-permute-start.7 = (bf16[4,2,144,128]{3,2,1,0:T(8,128)(2,1)S(1)}, bf16[4,2,144,128]{3,2,1,0:T(8,128)(2,1)S(1)}, u32[]{:S(2)}, u32[]{:S(2)}) collective-permute-start(bf16[4,2,144,128]{3,2,1,0:T(8,128)(2,1)S(1)} %get-tuple-element.29), channel_id=1, source_target_pairs={{0,62},{1,63},{2,0},{3,1},{4,2},{5,3},{6,4},{7,5},{8,6},{9,7},{10,... | collective-permute-start | bytes 884744 | tf_op jit(solution)/shard_map/ppermute | solution.py:213
  105.3 7.4 %attend.7.refs_2_ = bf16[8,2,144,128]{3,2,1,0:T(8,128)(2,1)S(1)} custom-call(s32[16,1]{1,0:T(8,128)S(1)} %copy.41.pos_new, bf16[2,2048,256]{2,1,0:T(8,128)(2,1)S(1)} %copy-done.3, bf16[2,128,2048]{2,1,0:T(8,128)(2,1)S(1)} %copy-done.4, bf16[2,16,128]{2,1,0:T(8,128)(2,1)S(1)} %get-tuple-element.71.new_k, bf16[2,16,128]{2,1,0:T(8,128)(2,1)S(1)} %get-tuple-element.70.new_v, ...), custom_call_target="tpu_custom_call" | custom-call | flops 3221225472 | bytes 4194304 | tf_op jit(solution)/shard_map/attend/pallas_call | solution.py:122
  112.8 0.8 copy-done.1
  113.6 0.7 copy-done.8
  114.4 0.7 copy-done.9
  115.1 3.1 %merge.5 = (bf16[8,2,144,128]{3,2,1,0:T(8,128)(2,1)}, bf16[8,2,144,128]{3,2,1,0:T(8,128)(2,1)}) custom-call(bf16[8,2,144,128]{3,2,1,0:T(8,128)(2,1)} %copy-done, bf16[4,2,144,128]{3,2,1,0:T(8,128)(2,1)} %copy-done.8, bf16[8,2,144,128]{3,2,1,0:T(8,128)(2,1)} %copy-done.1, bf16[4,2,144,128]{3,2,1,0:T(8,128)(2,1)} %copy-done.9), custom_call_target="tpu_custom_call" | custom-call | tf_op jit(solution)/shard_map/merge/pallas_call | solution.py:180
  118.2 2.7 collective-permute-start.10
  120.9 7.5 %collective-permute-done.9.refs_1_ = bf16[8,2,144,128]{3,2,1,0:T(8,128)(2,1)S(1)} collective-permute-done((bf16[8,2,144,128]{3,2,1,0:T(8,128)(2,1)}, bf16[8,2,144,128]{3,2,1,0:T(8,128)(2,1)S(1)}, u32[]{:S(2)}, u32[]{:S(2)}) %collective-permute-start.9) | collective-permute-done | bytes 589856 | tf_op jit(solution)/shard_map/ppermute | solution.py:213
  128.3 0.8 copy-done.6
  129.2 0.8 copy-done.7
  130.0 3.0 %merge.6 = bf16[8,2,144,128]{3,2,1,0:T(8,128)(2,1)} custom-call(bf16[8,2,144,128]{3,2,1,0:T(8,128)(2,1)} %copy-done.2, bf16[8,2,144,128]{3,2,1,0:T(8,128)(2,1)} %copy-done.6, bf16[8,2,144,128]{3,2,1,0:T(8,128)(2,1)} %copy-done.7), custom_call_target="tpu_custom_call" | custom-call | tf_op jit(solution)/shard_map/merge/pallas_call | solution.py:180
  133.0 0.8 constant_dynamic-slice_fusion.7
  133.8 1.2 collective-permute-start.11
  135.0 4.2 %collective-permute-start.12 = (bf16[1,1,144,128]{3,2,1,0:T(8,128)(2,1)S(1)}, bf16[1,1,144,128]{3,2,1,0:T(8,128)(2,1)S(1)}, u32[]{:S(2)}, u32[]{:S(2)}) collective-permute-start(bf16[1,1,144,128]{3,2,1,0:T(8,128)(2,1)S(1)} %get-tuple-element.49), channel_id=1, source_target_pairs={{0,56},{1,57},{2,58},{3,59},{4,60},{5,61},{6,62},{7,63},{8,0},{9,1... | collective-permute-start | bytes 110600 | tf_op jit(solution)/shard_map/ppermute | solution.py:213
  139.1 1.9 constant_dynamic-slice_fusion.4
  141.0 0.7 collective-permute-done.12.refs_3_
  141.7 0.6 copy-done.17
  142.3 1.6 merge.7
  143.9 4.5 %collective-permute-start.13 = (bf16[1,2,144,128]{3,2,1,0:T(8,128)(2,1)}, bf16[1,2,144,128]{3,2,1,0:T(8,128)(2,1)S(1)}, u32[]{:S(2)}, u32[]{:S(2)}) collective-permute-start(bf16[1,2,144,128]{3,2,1,0:T(8,128)(2,1)} %get-tuple-element.34), channel_id=1, source_target_pairs={{0,8},{1,9},{2,10},{3,11},{4,12},{5,13},{6,14},{7,15},{8,16},{9,17... | collective-permute-start | bytes 221192 | tf_op jit(solution)/shard_map/ppermute | solution.py:213
  148.5 0.9 collective-permute-start.14
  149.3 4.8 %collective-permute-done.13.refs_1_ = bf16[1,2,144,128]{3,2,1,0:T(8,128)(2,1)S(1)} collective-permute-done((bf16[1,2,144,128]{3,2,1,0:T(8,128)(2,1)}, bf16[1,2,144,128]{3,2,1,0:T(8,128)(2,1)S(1)}, u32[]{:S(2)}, u32[]{:S(2)}) %collective-permute-start.13) | collective-permute-done | bytes 73760 | tf_op jit(solution)/shard_map/ppermute | solution.py:213
  154.1 2.3 collective-permute-done.14.refs_3_
  156.4 0.6 copy-done.14
  157.0 1.7 merge.8
  158.7 2.7 %collective-permute-start.15 = (bf16[1,2,144,128]{3,2,1,0:T(8,128)(2,1)}, bf16[1,2,144,128]{3,2,1,0:T(8,128)(2,1)S(1)}, u32[]{:S(2)}, u32[]{:S(2)}) collective-permute-start(bf16[1,2,144,128]{3,2,1,0:T(8,128)(2,1)} %get-tuple-element.36), channel_id=1, source_target_pairs={{0,8},{1,9},{2,10},{3,11},{4,12},{5,13},{6,14},{7,15},{8,16},{9,17... | collective-permute-start | bytes 221192 | tf_op jit(solution)/shard_map/ppermute | solution.py:213
  161.4 2.6 collective-permute-start.16
  164.1 3.2 %collective-permute-done.15.refs_1_ = bf16[1,2,144,128]{3,2,1,0:T(8,128)(2,1)S(1)} collective-permute-done((bf16[1,2,144,128]{3,2,1,0:T(8,128)(2,1)}, bf16[1,2,144,128]{3,2,1,0:T(8,128)(2,1)S(1)}, u32[]{:S(2)}, u32[]{:S(2)}) %collective-permute-start.15) | collective-permute-done | bytes 73760 | tf_op jit(solution)/shard_map/ppermute | solution.py:213
  167.3 2.4 collective-permute-done.16.refs_3_
  169.7 0.6 copy-done.15
  170.3 1.7 merge.9
  172.0 2.4 collective-permute-start.17
  174.4 3.0 %collective-permute-start.18 = (bf16[1,2,144,128]{3,2,1,0:T(8,128)(2,1)}, bf16[1,2,144,128]{3,2,1,0:T(8,128)(2,1)S(1)}, u32[]{:S(2)}, u32[]{:S(2)}) collective-permute-start(bf16[1,2,144,128]{3,2,1,0:T(8,128)(2,1)} %get-tuple-element.39), channel_id=1, source_target_pairs={{0,56},{1,57},{2,58},{3,59},{4,60},{5,61},{6,62},{7,63},{8,0},{9,1... | collective-permute-start | bytes 221192 | tf_op jit(solution)/shard_map/ppermute | solution.py:213
  177.4 3.0 %collective-permute-done.17.refs_1_ = bf16[1,2,144,128]{3,2,1,0:T(8,128)(2,1)S(1)} collective-permute-done((bf16[1,2,144,128]{3,2,1,0:T(8,128)(2,1)}, bf16[1,2,144,128]{3,2,1,0:T(8,128)(2,1)S(1)}, u32[]{:S(2)}, u32[]{:S(2)}) %collective-permute-start.17) | collective-permute-done | bytes 73760 | tf_op jit(solution)/shard_map/ppermute | solution.py:213
  180.4 4.5 %collective-permute-done.18.refs_2_ = bf16[1,2,144,128]{3,2,1,0:T(8,128)(2,1)S(1)} collective-permute-done((bf16[1,2,144,128]{3,2,1,0:T(8,128)(2,1)}, bf16[1,2,144,128]{3,2,1,0:T(8,128)(2,1)S(1)}, u32[]{:S(2)}, u32[]{:S(2)}) %collective-permute-start.18) | collective-permute-done | bytes 73760 | tf_op jit(solution)/shard_map/ppermute | solution.py:213
  184.9 0.6 copy-done.11
  185.5 1.7 finish.1
  187.2 0.8 copy.63
  188.1 12.7 %collective-permute-start.19 = (bf16[4,4096]{1,0:T(4,128)(2,1)S(1)}, bf16[4,4096]{1,0:T(4,128)(2,1)S(1)}, u32[]{:S(2)}, u32[]{:S(2)}) collective-permute-start(bf16[4,4096]{1,0:T(4,128)(2,1)S(1)} %get-tuple-element.54), channel_id=1, source_target_pairs={{0,1},{1,0},{2,3},{3,2},{4,5},{5,4},{6,7},{7,6},{8,9},{9,8},{10,11... | collective-permute-start | bytes 98312 | tf_op jit(solution)/shard_map/ppermute | solution.py:216
  200.9 37.2 %all_gather.7 = bf16[8,8,4096]{2,1,0:T(8,128)(2,1)S(1)} all-gather(bf16[1,8,4096]{2,1,0:T(8,128)(2,1)S(1)} %all_gather_reshape.7), channel_id=1, replica_groups={{0,8,16,24,32,40,48,56},{1,9,17,25,33,41,49,57},{2,10,18,26,34,42,50,58..., dimensions={0}, use_global_device_ids=true | all-gather | bytes 589824 | tf_op jit(solution)/shard_map/all_gather | solution.py:233
  238.0 3.3 %collective-permute-start.20 = (bf16[8,8,4096]{2,1,0:T(8,128)(2,1)S(1)}, bf16[8,8,4096]{2,1,0:T(8,128)(2,1)S(1)}, u32[]{:S(2)}, u32[]{:S(2)}) collective-permute-start(bf16[8,8,4096]{2,1,0:T(8,128)(2,1)S(1)} %all_gather.7), channel_id=1, source_target_pairs={{0,62},{1,63},{2,0},{3,1},{4,2},{5,3},{6,4},{7,5},{8,6},{9,7},{10,... | collective-permute-start | bytes 1572872 | tf_op jit(solution)/shard_map/ppermute | solution.py:213
  241.3 0.7 maximum_select_fusion.1
  242.0 8.1 %collective-permute-done.20 = bf16[8,8,4096]{2,1,0:T(8,128)(2,1)S(1)} collective-permute-done((bf16[8,8,4096]{2,1,0:T(8,128)(2,1)S(1)}, bf16[8,8,4096]{2,1,0:T(8,128)(2,1)S(1)}, u32[]{:S(2)}, u32[]{:S(2)}) %collective-permute-start.20) | collective-permute-done | bytes 524320 | tf_op jit(solution)/shard_map/ppermute | solution.py:213
  250.1 2.8 %collective-permute-done.21 = bf16[8,8,4096]{2,1,0:T(8,128)(2,1)S(1)} collective-permute-done((bf16[8,8,4096]{2,1,0:T(8,128)(2,1)S(1)}, bf16[8,8,4096]{2,1,0:T(8,128)(2,1)S(1)}, u32[]{:S(2)}, u32[]{:S(2)}) %collective-permute-start.21) | collective-permute-done | bytes 524320 | tf_op jit(solution)/shard_map/ppermute | solution.py:213
  253.2 2.8 %collective-permute-start.22 = (bf16[4,8,4096]{2,1,0:T(8,128)(2,1)S(1)}, bf16[4,8,4096]{2,1,0:T(8,128)(2,1)S(1)}, u32[]{:S(2)}, u32[]{:S(2)}) collective-permute-start(bf16[4,8,4096]{2,1,0:T(8,128)(2,1)S(1)} %slice.54), channel_id=1, source_target_pairs={{0,62},{1,63},{2,0},{3,1},{4,2},{5,3},{6,4},{7,5},{8,6},{9,7},{10,... | collective-permute-start | bytes 786440 | tf_op jit(solution)/shard_map/ppermute | solution.py:213
  255.9 2.3 fusion.4
  258.3 1.3 collective-permute-done.23
  259.5 2.1 fusion.5
  261.6 5.2 %collective-permute-start.24 = (f32[256,256]{1,0:T(8,128)S(1)}, f32[256,256]{1,0:T(8,128)S(1)}, u32[]{:S(2)}, u32[]{:S(2)}) collective-permute-start(f32[256,256]{1,0:T(8,128)S(1)} %pad_maximum_fusion), channel_id=1, source_target_pairs={{0,1},{1,0},{2,3},{3,2},{4,5},{5,4},{6,7},{7,6},{8,9},{9,8},{10,11... | collective-permute-start | bytes 786440 | tf_op jit(solution)/shard_map/ppermute | solution.py:216
  268.1 0.7 copy.48
  (83 shorter events, 4.0 us)
Async XLA Ops:
  0.6 69.0 %collective-permute-start = (bf16[1024,1024]{1,0:T(8,128)(2,1)}, bf16[1024,1024]{1,0:T(8,128)(2,1)}, u32[]{:S(2)}, u32[]{:S(2)}) collective-permute-start(bf16[1024,1024]{1,0:T(8,128)(2,1)} %mine_v.1), channel_id=1, source_target_pairs={{0,1},{1,0},{2,3},{3,2},{4,5},{5,4},{6,7},{7,6},{8,9},{9,8},{10,11... | collective-permute-start | bytes 6291464 | tf_op jit(solution)/shard_map/ppermute | solution.py:216
  22.7 3.7 %copy-start.18 = (s32[256]{0:T(256)S(1)}, s32[256]{0:T(256)}, u32[]{:S(2)}) copy-start(s32[256]{0:T(256)} %param.9) | copy-start | bytes 3076
  22.7 4.1 %copy-start.19 = (s32[64]{0:T(128)S(1)}, s32[64]{0:T(128)}, u32[]{:S(2)}) copy-start(s32[64]{0:T(128)} %param.10) | copy-start | bytes 772
  22.7 6.9 %collective-permute-start.1 = (bf16[4,4608]{1,0:T(4,128)(2,1)S(1)}, bf16[4,4608]{1,0:T(4,128)(2,1)S(1)}, u32[]{:S(2)}, u32[]{:S(2)}) collective-permute-start(bf16[4,4608]{1,0:T(4,128)(2,1)S(1)} %pad_maximum_fusion.1), channel_id=1, source_target_pairs={{0,1},{1,0},{2,3},{3,2},{4,5},{5,4},{6,7},{7,6},{8,9},{9,8},{10,11... | collective-permute-start | bytes 110600 | tf_op jit(solution)/shard_map/ppermute | solution.py:216
  26.0 92.2 %collective-permute-start.8 = (bf16[4096,256]{1,0:T(8,128)(2,1)}, bf16[4096,256]{1,0:T(8,128)(2,1)}, u32[]{:S(2)}, u32[]{:S(2)}) collective-permute-start(bf16[4096,256]{1,0:T(8,128)(2,1)} %constant_dynamic-slice_fusion.12), channel_id=1, source_target_pairs={{0,1},{1,0},{2,3},{3,2},{4,5},{5,4},{6,7},{7,6},{8,9},{9,8},{10,11... | collective-permute-start | bytes 6291464 | tf_op jit(solution)/shard_map/ppermute | solution.py:216
  66.5 17.4 %collective-permute-start.2 = (bf16[8,2,128,128]{3,2,1,0:T(8,128)(2,1)S(1)}, bf16[8,2,128,128]{3,2,1,0:T(8,128)(2,1)S(1)}, u32[]{:S(2)}, u32[]{:S(2)}) collective-permute-start(bf16[8,2,128,128]{3,2,1,0:T(8,128)(2,1)S(1)} %all_gather.6.refs_0_), channel_id=1, source_target_pairs={{0,62},{1,63},{2,0},{3,1},{4,2},{5,3},{6,4},{7,5},{8,6},{9,7},{10,... | collective-permute-start | bytes 1572872 | tf_op jit(solution)/shard_map/ppermute | solution.py:213
  69.5 14.3 %collective-permute-start.3 = (bf16[8,2,128,128]{3,2,1,0:T(8,128)(2,1)S(1)}, bf16[8,2,128,128]{3,2,1,0:T(8,128)(2,1)S(1)}, u32[]{:S(2)}, u32[]{:S(2)}) collective-permute-start(bf16[8,2,128,128]{3,2,1,0:T(8,128)(2,1)S(1)} %all_gather.6.refs_0_), channel_id=1, source_target_pairs={{0,2},{1,3},{2,4},{3,5},{4,6},{5,7},{6,8},{7,9},{8,10},{9,11},{10,... | collective-permute-start | bytes 1572872 | tf_op jit(solution)/shard_map/ppermute | solution.py:213
  73.6 1.6 copy-start.3
  75.2 1.2 copy-start.4
  83.8 3.2 %copy-start.2 = (bf16[8,2,144,128]{3,2,1,0:T(8,128)(2,1)}, bf16[8,2,144,128]{3,2,1,0:T(8,128)(2,1)S(1)}, u32[]{:S(2)}) copy-start(bf16[8,2,144,128]{3,2,1,0:T(8,128)(2,1)S(1)} %attend.4.refs_0_) | copy-start | bytes 1769476
  83.9 11.4 %collective-permute-start.4 = (bf16[4,2,128,128]{3,2,1,0:T(8,128)(2,1)S(1)}, bf16[4,2,128,128]{3,2,1,0:T(8,128)(2,1)S(1)}, u32[]{:S(2)}, u32[]{:S(2)}) collective-permute-start(bf16[4,2,128,128]{3,2,1,0:T(8,128)(2,1)S(1)} %slice.46), channel_id=1, source_target_pairs={{0,62},{1,63},{2,0},{3,1},{4,2},{5,3},{6,4},{7,5},{8,6},{9,7},{10,... | collective-permute-start | bytes 786440 | tf_op jit(solution)/shard_map/ppermute | solution.py:213
  86.7 8.6 %collective-permute-start.5 = (bf16[4,2,128,128]{3,2,1,0:T(8,128)(2,1)S(1)}, bf16[4,2,128,128]{3,2,1,0:T(8,128)(2,1)S(1)}, u32[]{:S(2)}, u32[]{:S(2)}) collective-permute-start(bf16[4,2,128,128]{3,2,1,0:T(8,128)(2,1)S(1)} %slice.47), channel_id=1, source_target_pairs={{0,2},{1,3},{2,4},{3,5},{4,6},{5,7},{6,8},{7,9},{8,10},{9,11},{10,... | collective-permute-start | bytes 786440 | tf_op jit(solution)/shard_map/ppermute | solution.py:213
  94.5 0.8 copy-start
  102.5 11.1 %collective-permute-start.6 = (bf16[4,2,144,128]{3,2,1,0:T(8,128)(2,1)S(1)}, bf16[4,2,144,128]{3,2,1,0:T(8,128)(2,1)S(1)}, u32[]{:S(2)}, u32[]{:S(2)}) collective-permute-start(bf16[4,2,144,128]{3,2,1,0:T(8,128)(2,1)S(1)} %get-tuple-element.28), channel_id=1, source_target_pairs={{0,2},{1,3},{2,4},{3,5},{4,6},{5,7},{6,8},{7,9},{8,10},{9,11},{10,... | collective-permute-start | bytes 884744 | tf_op jit(solution)/shard_map/ppermute | solution.py:213
  102.6 11.0 %collective-permute-start.7 = (bf16[4,2,144,128]{3,2,1,0:T(8,128)(2,1)S(1)}, bf16[4,2,144,128]{3,2,1,0:T(8,128)(2,1)S(1)}, u32[]{:S(2)}, u32[]{:S(2)}) collective-permute-start(bf16[4,2,144,128]{3,2,1,0:T(8,128)(2,1)S(1)} %get-tuple-element.29), channel_id=1, source_target_pairs={{0,62},{1,63},{2,0},{3,1},{4,2},{5,3},{6,4},{7,5},{8,6},{9,7},{10,... | collective-permute-start | bytes 884744 | tf_op jit(solution)/shard_map/ppermute | solution.py:213
  112.8 0.8 copy-start.1
  113.6 0.8 copy-start.8
  114.4 0.7 copy-start.9
  118.2 10.2 %collective-permute-start.9 = (bf16[8,2,144,128]{3,2,1,0:T(8,128)(2,1)}, bf16[8,2,144,128]{3,2,1,0:T(8,128)(2,1)S(1)}, u32[]{:S(2)}, u32[]{:S(2)}) collective-permute-start(bf16[8,2,144,128]{3,2,1,0:T(8,128)(2,1)} %get-tuple-element.32), channel_id=1, source_target_pairs={{0,2},{1,3},{2,4},{3,5},{4,6},{5,7},{6,8},{7,9},{8,10},{9,11},{10,... | collective-permute-start | bytes 1769480 | tf_op jit(solution)/shard_map/ppermute | solution.py:213
  118.2 10.2 %collective-permute-start.10 = (bf16[8,2,144,128]{3,2,1,0:T(8,128)(2,1)}, bf16[8,2,144,128]{3,2,1,0:T(8,128)(2,1)S(1)}, u32[]{:S(2)}, u32[]{:S(2)}) collective-permute-start(bf16[8,2,144,128]{3,2,1,0:T(8,128)(2,1)} %get-tuple-element.33), channel_id=1, source_target_pairs={{0,62},{1,63},{2,0},{3,1},{4,2},{5,3},{6,4},{7,5},{8,6},{9,7},{10,... | collective-permute-start | bytes 1769480 | tf_op jit(solution)/shard_map/ppermute | solution.py:213
  128.3 0.8 copy-start.6
  129.1 0.8 copy-start.7
  133.8 7.3 %collective-permute-start.11 = (bf16[1,1,144,128]{3,2,1,0:T(8,128)(2,1)S(1)}, bf16[1,1,144,128]{3,2,1,0:T(8,128)(2,1)S(1)}, u32[]{:S(2)}, u32[]{:S(2)}) collective-permute-start(bf16[1,1,144,128]{3,2,1,0:T(8,128)(2,1)S(1)} %get-tuple-element.50), channel_id=1, source_target_pairs={{0,8},{1,9},{2,10},{3,11},{4,12},{5,13},{6,14},{7,15},{8,16},{9,17... | collective-permute-start | bytes 110600 | tf_op jit(solution)/shard_map/ppermute | solution.py:213
  135.0 6.7 %collective-permute-start.12 = (bf16[1,1,144,128]{3,2,1,0:T(8,128)(2,1)S(1)}, bf16[1,1,144,128]{3,2,1,0:T(8,128)(2,1)S(1)}, u32[]{:S(2)}, u32[]{:S(2)}) collective-permute-start(bf16[1,1,144,128]{3,2,1,0:T(8,128)(2,1)S(1)} %get-tuple-element.49), channel_id=1, source_target_pairs={{0,56},{1,57},{2,58},{3,59},{4,60},{5,61},{6,62},{7,63},{8,0},{9,1... | collective-permute-start | bytes 110600 | tf_op jit(solution)/shard_map/ppermute | solution.py:213
  141.0 0.7 copy-start.16
  141.7 0.6 copy-start.17
  143.9 10.1 %collective-permute-start.13 = (bf16[1,2,144,128]{3,2,1,0:T(8,128)(2,1)}, bf16[1,2,144,128]{3,2,1,0:T(8,128)(2,1)S(1)}, u32[]{:S(2)}, u32[]{:S(2)}) collective-permute-start(bf16[1,2,144,128]{3,2,1,0:T(8,128)(2,1)} %get-tuple-element.34), channel_id=1, source_target_pairs={{0,8},{1,9},{2,10},{3,11},{4,12},{5,13},{6,14},{7,15},{8,16},{9,17... | collective-permute-start | bytes 221192 | tf_op jit(solution)/shard_map/ppermute | solution.py:213
  148.5 7.9 %collective-permute-start.14 = (bf16[1,2,144,128]{3,2,1,0:T(8,128)(2,1)}, bf16[1,2,144,128]{3,2,1,0:T(8,128)(2,1)S(1)}, u32[]{:S(2)}, u32[]{:S(2)}) collective-permute-start(bf16[1,2,144,128]{3,2,1,0:T(8,128)(2,1)} %get-tuple-element.35), channel_id=1, source_target_pairs={{0,56},{1,57},{2,58},{3,59},{4,60},{5,61},{6,62},{7,63},{8,0},{9,1... | collective-permute-start | bytes 221192 | tf_op jit(solution)/shard_map/ppermute | solution.py:213
  154.1 2.3 copy-start.12
  156.4 0.6 copy-start.14
  158.7 8.6 %collective-permute-start.15 = (bf16[1,2,144,128]{3,2,1,0:T(8,128)(2,1)}, bf16[1,2,144,128]{3,2,1,0:T(8,128)(2,1)S(1)}, u32[]{:S(2)}, u32[]{:S(2)}) collective-permute-start(bf16[1,2,144,128]{3,2,1,0:T(8,128)(2,1)} %get-tuple-element.36), channel_id=1, source_target_pairs={{0,8},{1,9},{2,10},{3,11},{4,12},{5,13},{6,14},{7,15},{8,16},{9,17... | collective-permute-start | bytes 221192 | tf_op jit(solution)/shard_map/ppermute | solution.py:213
  161.4 8.2 %collective-permute-start.16 = (bf16[1,2,144,128]{3,2,1,0:T(8,128)(2,1)}, bf16[1,2,144,128]{3,2,1,0:T(8,128)(2,1)S(1)}, u32[]{:S(2)}, u32[]{:S(2)}) collective-permute-start(bf16[1,2,144,128]{3,2,1,0:T(8,128)(2,1)} %get-tuple-element.37), channel_id=1, source_target_pairs={{0,56},{1,57},{2,58},{3,59},{4,60},{5,61},{6,62},{7,63},{8,0},{9,1... | collective-permute-start | bytes 221192 | tf_op jit(solution)/shard_map/ppermute | solution.py:213
  167.3 2.4 copy-start.13
  169.7 0.6 copy-start.15
  172.0 8.3 %collective-permute-start.17 = (bf16[1,2,144,128]{3,2,1,0:T(8,128)(2,1)}, bf16[1,2,144,128]{3,2,1,0:T(8,128)(2,1)S(1)}, u32[]{:S(2)}, u32[]{:S(2)}) collective-permute-start(bf16[1,2,144,128]{3,2,1,0:T(8,128)(2,1)} %get-tuple-element.38), channel_id=1, source_target_pairs={{0,8},{1,9},{2,10},{3,11},{4,12},{5,13},{6,14},{7,15},{8,16},{9,17... | collective-permute-start | bytes 221192 | tf_op jit(solution)/shard_map/ppermute | solution.py:213
  174.4 10.5 %collective-permute-start.18 = (bf16[1,2,144,128]{3,2,1,0:T(8,128)(2,1)}, bf16[1,2,144,128]{3,2,1,0:T(8,128)(2,1)S(1)}, u32[]{:S(2)}, u32[]{:S(2)}) collective-permute-start(bf16[1,2,144,128]{3,2,1,0:T(8,128)(2,1)} %get-tuple-element.39), channel_id=1, source_target_pairs={{0,56},{1,57},{2,58},{3,59},{4,60},{5,61},{6,62},{7,63},{8,0},{9,1... | collective-permute-start | bytes 221192 | tf_op jit(solution)/shard_map/ppermute | solution.py:213
  180.4 4.5 %copy-start.10 = (bf16[1,2,144,128]{3,2,1,0:T(8,128)(2,1)}, bf16[1,2,144,128]{3,2,1,0:T(8,128)(2,1)S(1)}, u32[]{:S(2)}) copy-start(bf16[1,2,144,128]{3,2,1,0:T(8,128)(2,1)S(1)} %collective-permute-done.17.refs_1_) | copy-start | bytes 221188
  184.9 0.6 copy-start.11
  188.1 53.2 %collective-permute-start.19 = (bf16[4,4096]{1,0:T(4,128)(2,1)S(1)}, bf16[4,4096]{1,0:T(4,128)(2,1)S(1)}, u32[]{:S(2)}, u32[]{:S(2)}) collective-permute-start(bf16[4,4096]{1,0:T(4,128)(2,1)S(1)} %get-tuple-element.54), channel_id=1, source_target_pairs={{0,1},{1,0},{2,3},{3,2},{4,5},{5,4},{6,7},{7,6},{8,9},{9,8},{10,11... | collective-permute-start | bytes 98312 | tf_op jit(solution)/shard_map/ppermute | solution.py:216
  238.0 12.1 %collective-permute-start.20 = (bf16[8,8,4096]{2,1,0:T(8,128)(2,1)S(1)}, bf16[8,8,4096]{2,1,0:T(8,128)(2,1)S(1)}, u32[]{:S(2)}, u32[]{:S(2)}) collective-permute-start(bf16[8,8,4096]{2,1,0:T(8,128)(2,1)S(1)} %all_gather.7), channel_id=1, source_target_pairs={{0,62},{1,63},{2,0},{3,1},{4,2},{5,3},{6,4},{7,5},{8,6},{9,7},{10,... | collective-permute-start | bytes 1572872 | tf_op jit(solution)/shard_map/ppermute | solution.py:213
  241.3 11.7 %collective-permute-start.21 = (bf16[8,8,4096]{2,1,0:T(8,128)(2,1)S(1)}, bf16[8,8,4096]{2,1,0:T(8,128)(2,1)S(1)}, u32[]{:S(2)}, u32[]{:S(2)}) collective-permute-start(bf16[8,8,4096]{2,1,0:T(8,128)(2,1)S(1)} %all_gather.7), channel_id=1, source_target_pairs={{0,2},{1,3},{2,4},{3,5},{4,6},{5,7},{6,8},{7,9},{8,10},{9,11},{10,... | collective-permute-start | bytes 1572872 | tf_op jit(solution)/shard_map/ppermute | solution.py:213
  253.0 6.5 %collective-permute-start.23 = (bf16[4,8,4096]{2,1,0:T(8,128)(2,1)S(1)}, bf16[4,8,4096]{2,1,0:T(8,128)(2,1)S(1)}, u32[]{:S(2)}, u32[]{:S(2)}) collective-permute-start(bf16[4,8,4096]{2,1,0:T(8,128)(2,1)S(1)} %slice.55), channel_id=1, source_target_pairs={{0,2},{1,3},{2,4},{3,5},{4,6},{5,7},{6,8},{7,9},{8,10},{9,11},{10,... | collective-permute-start | bytes 786440 | tf_op jit(solution)/shard_map/ppermute | solution.py:213
  253.2 6.4 %collective-permute-start.22 = (bf16[4,8,4096]{2,1,0:T(8,128)(2,1)S(1)}, bf16[4,8,4096]{2,1,0:T(8,128)(2,1)S(1)}, u32[]{:S(2)}, u32[]{:S(2)}) collective-permute-start(bf16[4,8,4096]{2,1,0:T(8,128)(2,1)S(1)} %slice.54), channel_id=1, source_target_pairs={{0,62},{1,63},{2,0},{3,1},{4,2},{5,3},{6,4},{7,5},{8,6},{9,7},{10,... | collective-permute-start | bytes 786440 | tf_op jit(solution)/shard_map/ppermute | solution.py:213
  255.9 10.9 %copy-start.5 = (bf16[8192,256]{1,0:T(8,128)(2,1)S(1)}, bf16[8192,256]{1,0:T(8,128)(2,1)}, u32[]{:S(2)}) copy-start(bf16[8192,256]{1,0:T(8,128)(2,1)} %param.11) | copy-start | bytes 12582916
  261.6 6.3 %collective-permute-start.24 = (f32[256,256]{1,0:T(8,128)S(1)}, f32[256,256]{1,0:T(8,128)S(1)}, u32[]{:S(2)}, u32[]{:S(2)}) collective-permute-start(f32[256,256]{1,0:T(8,128)S(1)} %pad_maximum_fusion), channel_id=1, source_target_pairs={{0,1},{1,0},{2,3},{3,2},{4,5},{5,4},{6,7},{7,6},{8,9},{9,8},{10,11... | collective-permute-start | bytes 786440 | tf_op jit(solution)/shard_map/ppermute | solution.py:216
